TPU v7x, 32 devices: a 4x4x1 block of a 4x4x8 slice. The times are simulated.
32 devices in a mesh: rep: 1 (over z), mp: 4 (over y), tok: 8 (over x, core).
Axes of the slice: x: 4, y: 4, z: 1, core: 2. Of those that a mesh axis runs over, the one named last changes fastest.
The devices are a block of a 4x4x8 slice.
Arguments:
- hidden_in: bfloat16 [32768, 768], P(('rep', 'tok', 'mp'))
- seg_ids: int32 [32768], P(('rep', 'tok', 'mp'))
- expert_ids: int32 [32768, 2], P(('rep', 'tok', 'mp'))
- expert_gates: float32 [32768, 2], P(('rep', 'tok', 'mp'))
- w_query: bfloat16 [2, 768, 12, 64], P(None, 'tok', 'mp')
- w_key: bfloat16 [2, 768, 12, 64], P(None, 'tok', 'mp')
- w_value: bfloat16 [2, 768, 12, 64], P(None, 'tok', 'mp')
- w_out: bfloat16 [2, 12, 64, 768], P(None, 'mp', None, 'tok')
- w_gate: bfloat16 [2, 8, 768, 3072], P(None, None, 'tok', 'mp')
- w_up: bfloat16 [2, 8, 768, 3072], P(None, None, 'tok', 'mp')
- w_down: bfloat16 [2, 8, 3072, 768], P(None, None, 'mp', 'tok')
- gain_attn: bfloat16 [2, 768], replicated
- gain_mlp: bfloat16 [2, 768], replicated
Outputs:
- output: float32 [32768, 768], P(('rep', 'tok', 'mp'))
All inputs are finite; a program needn't handle non-finite values.
Results may differ from a plain program's by a relative error of at most 0.0101596.
Values are sent between devices in bfloat16 or wider.
A program may use at most 768 MiB of HBM per device.

v0:
```python
import jax
import jax.numpy as jnp
from jax import lax
from jax.sharding import PartitionSpec as P

EPS = 1e-5
ROPE_BASE = 10000.0


def rms_norm(residual, gain):
    inv_rms = lax.rsqrt(jnp.mean(residual * residual, axis=-1, keepdims=True) + EPS)
    return (residual * inv_rms * gain.astype(jnp.float32)).astype(jnp.bfloat16)


def request_positions(seg_rows):
    token_index = jnp.arange(seg_rows.shape[-1], dtype=jnp.int32)
    is_start = jnp.concatenate([jnp.ones(seg_rows.shape[:-1] + (1,), dtype=jnp.bool_), seg_rows[..., 1:] != seg_rows[..., :-1]], axis=-1)
    start_index = lax.cummax(jnp.where(is_start, token_index, 0), axis=seg_rows.ndim - 1)
    return token_index - start_index


def rope_tables(positions, head_dim):
    inv_freq = jnp.power(ROPE_BASE, -jnp.arange(head_dim // 2, dtype=jnp.float32) * 2.0 / head_dim)
    angles = positions.astype(jnp.float32)[..., None] * inv_freq
    return jnp.cos(angles)[..., None, :], jnp.sin(angles)[..., None, :]


def apply_rope(vectors, cosines, sines):
    half_dim = vectors.shape[-1] // 2
    first_half = vectors[..., :half_dim]
    second_half = vectors[..., half_dim:]
    return jnp.concatenate([first_half * cosines - second_half * sines, second_half * cosines + first_half * sines], axis=-1)


def block_attention(q_rot, k_rot, v_all, seg_query, query_index, seg_keys, key_index):
    n_query, kv_heads, groups, head_dim = q_rot.shape
    block = min(n_query, 512)
    num_blocks = n_query // block
    scale = head_dim ** -0.5

    def one_block(block_in):
        q_block, seg_block, index_block = block_in
        scores = jnp.einsum('bhgd,shd->hgbs', q_block, k_rot, preferred_element_type=jnp.float32) * scale
        allowed = (seg_block[:, None] == seg_keys[None, :]) & (key_index[None, :] <= index_block[:, None])
        attn_prob = jax.nn.softmax(jnp.where(allowed, scores, -1e30), axis=-1).astype(jnp.bfloat16)
        return jnp.einsum('hgbs,shd->bhgd', attn_prob, v_all, preferred_element_type=jnp.float32).astype(jnp.bfloat16)

    block_outs = lax.map(one_block, (q_rot.reshape(num_blocks, block, kv_heads, groups, head_dim), seg_query.reshape(num_blocks, block), query_index.reshape(num_blocks, block)))
    return block_outs.reshape(n_query, kv_heads * groups, head_dim)


def expert_mix(normed, pair_token, pair_gate, group_sizes, gate_weight, up_weight, down_weight):
    pair_rows = normed[pair_token]
    gate_pre = lax.ragged_dot(pair_rows, gate_weight, group_sizes, preferred_element_type=jnp.float32)
    up_pre = lax.ragged_dot(pair_rows, up_weight, group_sizes, preferred_element_type=jnp.float32)
    hidden_act = (jax.nn.silu(gate_pre) * up_pre).astype(jnp.bfloat16)
    down_out = lax.ragged_dot(hidden_act, down_weight, group_sizes, preferred_element_type=jnp.float32)
    return jax.ops.segment_sum(down_out * pair_gate[:, None], pair_token, num_segments=normed.shape[0])


def solution(mesh):
    token_spec = P(('rep', 'tok', 'mp'))
    row_spec = P(('rep', 'tok', 'mp'), None)
    head_weight = P(None, 'tok', 'mp', None)
    in_specs = (row_spec, token_spec, row_spec, row_spec, head_weight, head_weight, head_weight, P(None, 'mp', None, 'tok'), P(None, None, 'tok', 'mp'), P(None, None, 'tok', 'mp'), P(None, None, 'mp', 'tok'), P(None, None), P(None, None))

    def device_step(hidden_in, seg_ids, expert_ids, expert_gates, w_query, w_key, w_value, w_out, w_gate, w_up, w_down, gain_attn, gain_mlp):
        num_layers, _, q_local, head_dim = w_query.shape
        kv_local = w_key.shape[2]
        groups = q_local // kv_local
        num_experts = w_gate.shape[1]
        seg_full = lax.all_gather(seg_ids, 'mp', axis=0, tiled=True)
        ids_full = lax.all_gather(expert_ids, 'mp', axis=0, tiled=True)
        gates_full = lax.all_gather(expert_gates, 'mp', axis=0, tiled=True)
        seq_len = seg_full.shape[0]
        token_index = jnp.arange(seq_len, dtype=jnp.int32)
        cosines, sines = rope_tables(request_positions(seg_full), head_dim)
        flat_ids = ids_full.reshape(2 * seq_len)
        pair_order = jnp.argsort(flat_ids, stable=True)
        group_sizes = jnp.bincount(flat_ids, length=num_experts).astype(jnp.int32)
        pair_token = pair_order // 2
        pair_gate = gates_full.reshape(2 * seq_len)[pair_order]
        residual = hidden_in.astype(jnp.float32)
        for layer in range(num_layers):
            q_weight = lax.all_gather(w_query[layer], 'tok', axis=0, tiled=True)
            k_weight = lax.all_gather(w_key[layer], 'tok', axis=0, tiled=True)
            v_weight = lax.all_gather(w_value[layer], 'tok', axis=0, tiled=True)
            o_weight = lax.all_gather(w_out[layer], 'tok', axis=2, tiled=True)
            gate_weight = lax.all_gather(w_gate[layer], 'tok', axis=1, tiled=True)
            up_weight = lax.all_gather(w_up[layer], 'tok', axis=1, tiled=True)
            down_weight = lax.all_gather(w_down[layer], 'tok', axis=2, tiled=True)
            normed = lax.all_gather(rms_norm(residual, gain_attn[layer]), 'mp', axis=0, tiled=True)
            q_proj = jnp.einsum('se,ehd->shd', normed, q_weight, preferred_element_type=jnp.float32)
            k_proj = jnp.einsum('se,ehd->shd', normed, k_weight, preferred_element_type=jnp.float32)
            v_proj = jnp.einsum('se,ehd->shd', normed, v_weight, preferred_element_type=jnp.float32)
            q_rot = apply_rope(q_proj, cosines, sines).astype(jnp.bfloat16).reshape(seq_len, kv_local, groups, head_dim)
            k_rot = apply_rope(k_proj, cosines, sines).astype(jnp.bfloat16)
            attn_out = block_attention(q_rot, k_rot, v_proj.astype(jnp.bfloat16), seg_full, token_index, seg_full, token_index)
            attn_part = jnp.einsum('shd,hde->se', attn_out, o_weight, preferred_element_type=jnp.float32)
            residual = residual + lax.psum_scatter(attn_part, 'mp', scatter_dimension=0, tiled=True)
            normed = lax.all_gather(rms_norm(residual, gain_mlp[layer]), 'mp', axis=0, tiled=True)
            mix_part = expert_mix(normed, pair_token, pair_gate, group_sizes, gate_weight, up_weight, down_weight)
            residual = residual + lax.psum_scatter(mix_part, 'mp', scatter_dimension=0, tiled=True)
        return residual

    return jax.shard_map(device_step, mesh=mesh, in_specs=in_specs, out_specs=row_spec, check_vma=False)
```

profile of v0, /device:TPU:97, one launch (start us, length us, event | category | flops | bytes accessed | tf_op | source)
XLA Modules:
  0.0 2120.9 jit_solution(10967181566360262413)
XLA Ops:
  26.8 22.9 %all-gather = bf16[1,768,3,64]{3,2,0,1:T(4,128)(2,1)S(1)} all-gather(bf16[1,96,3,64]{3,2,0,1:T(4,128)(2,1)S(1)} %copy.60), channel_id=2, replica_groups=mesh['rep'=1,'mp'=4,'tok'=8] {'tok'}, dimensions={1}, use_global_device_ids=true | all-gather | bytes 331776 | tf_op jit(solution)/shard_map/all_gather | solution.py:85
  51.0 24.2 %all-gather.1 = bf16[1,768,3,64]{3,2,0,1:T(4,128)(2,1)S(1)} all-gather(bf16[1,96,3,64]{3,2,0,1:T(4,128)(2,1)S(1)} %copy.61), channel_id=3, replica_groups=mesh['rep'=1,'mp'=4,'tok'=8] {'tok'}, dimensions={1}, use_global_device_ids=true | all-gather | bytes 331776 | tf_op jit(solution)/shard_map/all_gather | solution.py:86
  98.5 23.2 %all-gather.3 = bf16[1,3,64,768]{2,1,0,3:T(4,128)(2,1)S(1)} all-gather(bf16[1,3,64,96]{2,1,0,3:T(4,128)(2,1)S(1)} %copy.63), channel_id=5, replica_groups=mesh['rep'=1,'mp'=4,'tok'=8] {'tok'}, dimensions={3}, use_global_device_ids=true | all-gather | bytes 331776 | tf_op jit(solution)/shard_map/all_gather | solution.py:88
  139.7 307.7 %while.22 = (s32[]{:T(128)}, bf16[8,512,3,1,64]{1,4,2,3,0:T(8,128)(2,1)S(1)}, s32[8,512]{1,0:T(8,128)S(1)}, s32[4096]{0:T(1024)S(1)}, s32[8,512]{1,0:T(8,128)S(1...) while((s32[]{:T(128)}, ...), condition=%wide.region_6.7_spmd.clone, body=%wide.region_3.6_spmd.clone.sunk | while | flops 1692496896 | bytes 93780608 | solution.py:48
  463.2 112.5 %reduce-scatter.5.cloned.1.call-done = f32[1024,768]{1,0:T(8,128)} async-done(((f32[4096,768]{1,0:T(8,128)}), f32[1024,768]{1,0:T(8,128)}) %reduce-scatter.5.cloned.1.call-update) | async-done | bytes 3145744 | tf_op jit(solution)/shard_map/reduce_scatter | solution.py:100
  606.5 57.5 %scatter_custom_fusion = s32[8]{0:T(128)} fusion(s32[8192]{0:T(1024)S(1)} %reshape.312, s32[8192]{0:T(1024)S(1)} %ne.20, s32[]{:T(128)} %copy.89), kind=kCustom, calls=%fused_computation.117 | custom fusion | flops 8192 | bytes 36 | tf_op jit(solution)/shard_map/scatter-add | solution.py:80
  687.7 45.5 %gather_fusion.1 = f32[8192]{0:T(1024)S(1)} fusion(f32[8192]{0:T(1024)S(1)} %reshape.280, s32[8192]{0:T(1024)S(1)} %get-tuple-element.237), kind=kCustom, calls=%fused_computation.1 | custom fusion | bytes 98304 | tf_op jit(solution)/shard_map/gather | solution.py:82
  746.1 40.6 %gather_fusion = bf16[8192,768]{1,0:T(8,128)(2,1)} fusion(bf16[4096,768]{1,0:T(8,128)(2,1)} %all-gather.27.cloned.1.call-done, s32[8192]{0:T(1024)S(1)} %get-tuple-element.238), kind=kCustom, calls=%fused_computation | custom fusion | bytes 25198592 | tf_op jit(solution)/shard_map/gather | solution.py:53
  786.7 39.4 %ragged-dot-none.5 = f32[8192,768]{1,0:T(8,128)} custom-call(s32[1]{0:T(128)} %get-tuple-element.115, s32[9]{0:T(128)} %get-tuple-element.116, s32[39]{0:T(128)} %get-tuple-element.117, s32[39]{0:T(128)} %get-tuple-element.118, s32[1]{0:T(128)} %get-tuple-element.115, bf16[8192,768]{1,0:T(8,128)(2,1)} %gather_fusion, bf16[8,768,768]{2,1,0:T(8,128)(2,1)} %bitcast.240), custom_call_target="tpu_custom_call" | custom-call | flops 9663676416 | bytes 47185952 | tf_op jit(solution)/shard_map/ragged_dot_general/ragged-dot-none
  826.1 39.3 %ragged-dot-none.4 = f32[8192,768]{1,0:T(8,128)} custom-call(s32[1]{0:T(128)} %get-tuple-element.115, s32[9]{0:T(128)} %get-tuple-element.116, s32[39]{0:T(128)} %get-tuple-element.117, s32[39]{0:T(128)} %get-tuple-element.118, s32[1]{0:T(128)} %get-tuple-element.115, bf16[8192,768]{1,0:T(8,128)(2,1)} %gather_fusion, bf16[8,768,768]{2,1,0:T(8,128)(2,1)} %bitcast.241), custom_call_target="tpu_custom_call" | custom-call | flops 9663676416 | bytes 47185952 | tf_op jit(solution)/shard_map/ragged_dot_general/ragged-dot-none
  887.1 39.6 %ragged-dot-none.3 = f32[8192,768]{1,0:T(8,128)} custom-call(s32[1]{0:T(128)} %get-tuple-element.115, s32[9]{0:T(128)} %get-tuple-element.116, s32[39]{0:T(128)} %get-tuple-element.117, s32[39]{0:T(128)} %get-tuple-element.118, s32[1]{0:T(128)} %get-tuple-element.115, bf16[8192,768]{1,0:T(8,128)(2,1)} %multiply_convert_fusion.1, bf16[8,768,768]{2,1,0:T(8,128)(2,1)} %bitcast.233), custom_call_target="tpu_custom_call" | custom-call | flops 9663676416 | bytes 47185952 | tf_op jit(solution)/shard_map/ragged_dot_general/ragged-dot-none
  926.7 63.3 %scatter_custom_fusion.1 = f32[4096,768]{1,0:T(8,128)} fusion(s32[8192]{0:T(1024)S(1)} %get-tuple-element.239, f32[8192,768]{1,0:T(8,128)} %ragged-dot-none.3, f32[8192]{0:T(1024)S(1)} %gather_fusion.1, f32[]{:T(128)} %constant.82.clone.1), kind=kCustom, calls=%fused_computation.51 | custom fusion | flops 12582912 | bytes 37781508 | tf_op jit(solution)/shard_map/scatter-add | solution.py:58
  990.2 116.8 %reduce-scatter.7.cloned.1.call-done = f32[1024,768]{1,0:T(8,128)} async-done(((f32[4096,768]{1,0:T(8,128)}), f32[1024,768]{1,0:T(8,128)}) %reduce-scatter.7.cloned.1.call-update) | async-done | bytes 3145744 | tf_op jit(solution)/shard_map/reduce_scatter | solution.py:103
  1134.5 23.9 %all-gather.8 = bf16[1,768,3,64]{3,2,0,1:T(4,128)(2,1)S(1)} all-gather(bf16[1,96,3,64]{3,2,0,1:T(4,128)(2,1)S(1)} %copy.66), channel_id=10, replica_groups=mesh['rep'=1,'mp'=4,'tok'=8] {'tok'}, dimensions={1}, use_global_device_ids=true | all-gather | bytes 331776 | tf_op jit(solution)/shard_map/all_gather | solution.py:86
  1182.0 22.2 %all-gather.10 = bf16[1,3,64,768]{2,1,0,3:T(4,128)(2,1)S(1)} all-gather(bf16[1,3,64,96]{2,1,0,3:T(4,128)(2,1)S(1)} %copy.68), channel_id=12, replica_groups=mesh['rep'=1,'mp'=4,'tok'=8] {'tok'}, dimensions={3}, use_global_device_ids=true | all-gather | bytes 331776 | tf_op jit(solution)/shard_map/all_gather | solution.py:88
  1219.8 313.3 %while.23 = (s32[]{:T(128)}, bf16[8,512,3,1,64]{1,4,2,3,0:T(8,128)(2,1)S(1)}, s32[8,512]{1,0:T(8,128)}, s32[4096]{0:T(1024)S(1)}, s32[8,512]{1,0:T(8,128)}, /*in...) while((s32[]{:T(128)}, ...), condition=%wide.region_17.18_spmd.clone, body=%wide.region_14.17_spmd.clone.sunk | while | flops 1692496896 | bytes 93780608 | solution.py:48
  1544.8 112.4 %reduce-scatter.9.cloned.1.call-done = f32[1024,768]{1,0:T(8,128)} async-done(((f32[4096,768]{1,0:T(8,128)}), f32[1024,768]{1,0:T(8,128)}) %reduce-scatter.9.cloned.1.call-update) | async-done | bytes 3145744 | tf_op jit(solution)/shard_map/reduce_scatter | solution.py:100
  1677.0 48.7 %all-gather.31.cloned.1.call-done = bf16[4096,768]{1,0:T(8,128)(2,1)} async-done(((bf16[1024,768]{1,0:T(8,128)(2,1)}), bf16[4096,768]{1,0:T(8,128)(2,1)}) %all-gather.31.cloned.1.call-update) | async-done | bytes 6291472 | tf_op jit(solution)/shard_map/all_gather | solution.py:101
  1725.7 40.6 %gather_fusion.2 = bf16[8192,768]{1,0:T(8,128)(2,1)} fusion(bf16[4096,768]{1,0:T(8,128)(2,1)} %all-gather.31.cloned.1.call-done, s32[8192]{0:T(1024)S(1)} %copy-done.21), kind=kCustom, calls=%fused_computation.2 | custom fusion | bytes 25198592 | tf_op jit(solution)/shard_map/gather | solution.py:53
  1779.9 39.4 %ragged-dot-none.2 = f32[8192,768]{1,0:T(8,128)} custom-call(s32[1]{0:T(128)} %get-tuple-element.115, s32[9]{0:T(128)} %get-tuple-element.116, s32[39]{0:T(128)} %get-tuple-element.117, s32[39]{0:T(128)} %get-tuple-element.118, s32[1]{0:T(128)} %get-tuple-element.115, bf16[8192,768]{1,0:T(8,128)(2,1)} %gather_fusion.2, bf16[8,768,768]{2,1,0:T(8,128)(2,1)} %bitcast.242), custom_call_target="tpu_custom_call" | custom-call | flops 9663676416 | bytes 47185952 | tf_op jit(solution)/shard_map/ragged_dot_general/ragged-dot-none
  1833.0 39.3 %ragged-dot-none.1 = f32[8192,768]{1,0:T(8,128)} custom-call(s32[1]{0:T(128)} %get-tuple-element.115, s32[9]{0:T(128)} %get-tuple-element.116, s32[39]{0:T(128)} %get-tuple-element.117, s32[39]{0:T(128)} %get-tuple-element.118, s32[1]{0:T(128)} %get-tuple-element.115, bf16[8192,768]{1,0:T(8,128)(2,1)} %gather_fusion.2, bf16[8,768,768]{2,1,0:T(8,128)(2,1)} %bitcast.243), custom_call_target="tpu_custom_call" | custom-call | flops 9663676416 | bytes 47185952 | tf_op jit(solution)/shard_map/ragged_dot_general/ragged-dot-none
  1893.9 39.4 %ragged-dot-none = f32[8192,768]{1,0:T(8,128)} custom-call(s32[1]{0:T(128)} %get-tuple-element.115, s32[9]{0:T(128)} %get-tuple-element.116, s32[39]{0:T(128)} %get-tuple-element.117, s32[39]{0:T(128)} %get-tuple-element.118, s32[1]{0:T(128)} %get-tuple-element.115, bf16[8192,768]{1,0:T(8,128)(2,1)} %multiply_convert_fusion, bf16[8,768,768]{2,1,0:T(8,128)(2,1)} %bitcast.232), custom_call_target="tpu_custom_call" | custom-call | flops 9663676416 | bytes 47185952 | tf_op jit(solution)/shard_map/ragged_dot_general/ragged-dot-none
  1933.4 63.3 %scatter_custom_fusion.2 = f32[4096,768]{1,0:T(8,128)} fusion(s32[8192]{0:T(1024)} %copy-done.32, f32[8192,768]{1,0:T(8,128)} %ragged-dot-none, f32[8192]{0:T(1024)S(1)} %copy-done.19, f32[]{:T(128)} %constant.82.clone.1), kind=kCustom, calls=%fused_computation.48 | custom fusion | flops 12582912 | bytes 37782016 | tf_op jit(solution)/shard_map/scatter-add | solution.py:58
  1996.7 112.7 %reduce-scatter.11.cloned.1.call-done = f32[1024,768]{1,0:T(8,128)} async-done(((f32[4096,768]{1,0:T(8,128)}), f32[1024,768]{1,0:T(8,128)}) %reduce-scatter.11.cloned.1.call-update) | async-done | bytes 3145744 | tf_op jit(solution)/shard_map/reduce_scatter | solution.py:103
  (326 shorter events, 936.8 us)
Async XLA Ops:
  7.4 117.5 %all-gather.25.cloned.1.call-start = ((), (), s32[]{:S(2)}) async-start(), calls=%async_computation.4 | async-start | bytes 7864320 | tf_op jit(solution)/shard_map/all_gather | solution.py:92
  13.7 562.0 %reduce-scatter.5.cloned.1.call-start = ((), (), s32[]{:S(2)}) async-start(), calls=%async_computation.5 | async-start | bytes 15728640 | tf_op jit(solution)/shard_map/reduce_scatter | solution.py:100
  26.7 71.0 %copy-start.29 = (bf16[2,3,64,96]{3,2,1,0:T(8,128)(2,1)S(1)}, bf16[2,3,64,96]{3,2,1,0:T(8,128)(2,1)}, u32[]{:S(2)}) copy-start(bf16[2,3,64,96]{3,2,1,0:T(8,128)(2,1)} %param.24) | copy-start | bytes 221188
  457.8 118.0 %copy-start.2 = (bf16[1024,768]{1,0:T(8,128)(2,1)S(1)}, bf16[1024,768]{1,0:T(8,128)(2,1)}, u32[]{:S(2)}) copy-start(bf16[1024,768]{1,0:T(8,128)(2,1)} %param.17) | copy-start | bytes 4718596
  457.8 275.5 %all-gather.37.cloned.1.call-start = ((), (), s32[]{:S(2)}) async-start(), calls=%async_computation.14 | async-start | bytes 10616832 | tf_op jit(solution)/shard_map/all_gather | solution.py:91
  462.5 283.6 %all-gather.27.cloned.1.call-start = ((), (), s32[]{:S(2)}) async-start(), calls=%async_computation.6 | async-start | bytes 7864320 | tf_op jit(solution)/shard_map/all_gather | solution.py:101
  580.3 206.4 %all-gather.33.cloned.1.call-start = ((), (), s32[]{:S(2)}) async-start(), calls=%async_computation.12 | async-start | bytes 10616832 | tf_op jit(solution)/shard_map/all_gather | solution.py:89
  583.7 242.5 %all-gather.35.cloned.1.call-start = ((), (), s32[]{:S(2)}) async-start(), calls=%async_computation.13 | async-start | bytes 10616832 | tf_op jit(solution)/shard_map/all_gather | solution.py:90
  587.0 519.9 %reduce-scatter.7.cloned.1.call-start = ((), (), s32[]{:S(2)}) async-start(), calls=%async_computation.7 | async-start | bytes 15728640 | tf_op jit(solution)/shard_map/reduce_scatter | solution.py:103
  599.0 66.7 %copy-start.37 = (f32[1024,2]{0,1:T(2,128)S(1)}, f32[1024,2]{0,1:T(2,128)}, u32[]{:S(2)}) copy-start(f32[1024,2]{0,1:T(2,128)} %param.20) | copy-start | bytes 24580
  687.7 239.0 %copy-start.32 = (s32[8192]{0:T(1024)}, s32[8192]{0:T(1024)S(1)}, u32[]{:S(2)}) copy-start(s32[8192]{0:T(1024)S(1)} %get-tuple-element.239) | copy-start | bytes 98308
  733.2 193.5 %copy-start.18 = (f32[8192]{0:T(1024)}, f32[8192]{0:T(1024)S(1)}, u32[]{:S(2)}) copy-start(f32[8192]{0:T(1024)S(1)} %gather_fusion.1) | copy-start | bytes 98308
  990.1 122.0 %copy-start.33 = (f32[768]{0:T(1024)S(1)}, f32[768]{0:T(1024)}, u32[]{:S(2)}) copy-start(f32[768]{0:T(1024)} %get-tuple-element.165) | copy-start | bytes 9220
  990.1 215.2 %all-gather.29.cloned.1.call-start = ((), (), s32[]{:S(2)}) async-start(), calls=%async_computation.8 | async-start | bytes 7864320 | tf_op jit(solution)/shard_map/all_gather | solution.py:92
  1113.6 543.7 %reduce-scatter.9.cloned.1.call-start = ((), (), s32[]{:S(2)}) async-start(), calls=%async_computation.9 | async-start | bytes 15728640 | tf_op jit(solution)/shard_map/reduce_scatter | solution.py:100
  1113.7 68.1 %copy-start.25 = (bf16[1,3,64,96]{3,2,1,0:T(8,128)(2,1)S(1)}, bf16[1,3,64,96]{3,2,1,0:T(8,128)(2,1)}, u32[]{:S(2)}) copy-start(bf16[1,3,64,96]{3,2,1,0:T(8,128)(2,1)} %get-tuple-element.229) | copy-start | bytes 110596
  1541.3 116.0 %copy-start.4 = (f32[1024,768]{1,0:T(8,128)S(1)}, f32[1024,768]{1,0:T(8,128)}, u32[]{:S(2)}) copy-start(f32[1024,768]{1,0:T(8,128)} %copy-done.3) | copy-start | bytes 9437188
  1541.3 122.9 %all-gather.43.cloned.1.call-start = ((), (), s32[]{:S(2)}) async-start(), calls=%async_computation.17 | async-start | bytes 10616832 | tf_op jit(solution)/shard_map/all_gather | solution.py:91
  1544.7 116.5 %copy-start.34 = (f32[768]{0:T(1024)S(1)}, f32[768]{0:T(1024)}, u32[]{:S(2)}) copy-start(f32[768]{0:T(1024)} %get-tuple-element.163) | copy-start | bytes 9220
  1544.8 181.0 %all-gather.31.cloned.1.call-start = ((), (), s32[]{:S(2)}) async-start(), calls=%async_computation.10 | async-start | bytes 7864320 | tf_op jit(solution)/shard_map/all_gather | solution.py:101
  1662.8 117.0 %all-gather.39.cloned.1.call-start = ((), (), s32[]{:S(2)}) async-start(), calls=%async_computation.15 | async-start | bytes 10616832 | tf_op jit(solution)/shard_map/all_gather | solution.py:89
  1663.5 169.5 %all-gather.41.cloned.1.call-start = ((), (), s32[]{:S(2)}) async-start(), calls=%async_computation.16 | async-start | bytes 10616832 | tf_op jit(solution)/shard_map/all_gather | solution.py:90
  1664.1 445.2 %reduce-scatter.11.cloned.1.call-start = ((), (), s32[]{:S(2)}) async-start(), calls=%async_computation.11 | async-start | bytes 15728640 | tf_op jit(solution)/shard_map/reduce_scatter | solution.py:103
  1996.7 112.7 %copy-start.7 = (f32[1024,768]{1,0:T(8,128)S(1)}, f32[1024,768]{1,0:T(8,128)}, u32[]{:S(2)}) copy-start(f32[1024,768]{1,0:T(8,128)} %copy-done.6) | copy-start | bytes 9437188
  (43 other events, 595.4 us)
Sparse Core Ops, SparseCore 0:
  13.8 66.9 all-gather.24
  457.9 117.8 reduce-scatter.4
  990.2 116.6 reduce-scatter.6
  1541.4 115.8 reduce-scatter.8
  1996.8 112.4 reduce-scatter.10
Sparse Core Ops, SparseCore 1:
  462.6 57.7 all-gather.36
  580.4 63.1 all-gather.26
  645.0 52.4 all-gather.32
  699.1 51.6 all-gather.34
  1113.7 62.7 all-gather.28
  1544.8 55.8 all-gather.42
  1662.9 62.7 all-gather.30
  1727.2 52.6 all-gather.38
  1781.3 51.6 all-gather.40
where the time goes:
time: 2130 us; the launch traced here: 2120 us
  waiting for transfers between devices  532 us (25%)
  other arithmetic  502 us (24%)
  matrix products  412 us (19%)
  Pallas kernels  238 us (11%)
  blocking collectives  211 us (10%)
  local copies, waits for them, and re-layouts  207 us (10%)
    another operation x6, Pallas kernels  237 us
    reduce_scatter x2, waiting for transfers between devices, device_step(): lax.psum_scatter(mix_part, 'mp', scatter_dimension=0, tiled=True)  229 us
    reduce_scatter x2, waiting for transfers between devices, device_step(): lax.psum_scatter(attn_part, 'mp', scatter_dimension=0, tiled=True)  225 us
    dot_general x16, matrix products, one_block(): jnp.einsum('hgbs,shd->bhgd', attn_prob, v_all, preferred_element_type=jnp...  193 us
    reduce_sum x16, other arithmetic, one_block(): jax.nn.softmax(jnp.where(allowed, scores, -1e+30), axis=-1)  191 us
    dot_general x16, matrix products, one_block(): jnp.einsum('bhgd,shd->hgbs', q_block, k_rot, preferred_element_type=jnp.f...  187 us
    scatter-add x2, other arithmetic, expert_mix(): jax.ops.segment_sum(down_out * pair_gate[:, None], pair_token, num_segmen...  127 us
    gather x2, local copies, waits for them, and re-layouts, expert_mix(): pair_rows = normed[pair_token]  81.3 us
  transfers between devices with their start and end apart: 14, of which 7 were waited for; matrix products, arithmetic and copies ran while one was open for 12% of the time, Pallas kernels for 4%

commit v1 on v0

v1 whole, which is shorter than its diff:
```python
import functools

import jax
import jax.numpy as jnp
from jax import lax
from jax.experimental import pallas as pl
from jax.experimental.pallas import tpu as pltpu
from jax.sharding import PartitionSpec as P


EPS = 1e-5
ROPE_BASE = 10000.0
NEG = -1e30
VMEM_LIMIT = 60 * 1024 * 1024
F32 = jnp.float32
BF16 = jnp.bfloat16
NT = (((1,), (1,)), ((), ()))


def rms_norm(residual, gain):
    inv_rms = lax.rsqrt(jnp.mean(residual * residual, axis=-1, keepdims=True) + EPS)
    return (residual * inv_rms * gain.astype(F32)).astype(BF16)


def request_starts(seg_rows):
    token_index = jnp.arange(seg_rows.shape[0], dtype=jnp.int32)
    is_start = jnp.concatenate([jnp.ones((1,), dtype=jnp.bool_), seg_rows[1:] != seg_rows[:-1]])
    return lax.cummax(jnp.where(is_start, token_index, 0), axis=0)


def attention_kernel(heads, head_dim, bounds_ref, h_ref, w_ref, cos_ref, sin_ref, start_ref, out_ref, q_sc, k_sc, v_sc, m_sc, l_sc, acc_sc):
    tile = pl.program_id(0)
    rows = h_ref.shape[0]
    width = heads * head_dim
    half = head_dim // 2
    qkv = lax.dot_general(w_ref[...], h_ref[...], NT, preferred_element_type=F32)
    cosines = cos_ref[...]
    sines = sin_ref[...]

    def rotate(base):
        first = qkv[base:base + half]
        second = qkv[base + half:base + head_dim]
        return jnp.concatenate([first * cosines - second * sines, second * cosines + first * sines], axis=0)

    scale = head_dim ** -0.5
    for head in range(heads):
        base = head * head_dim
        q_sc[head] = (rotate(base).astype(BF16).astype(F32) * scale).astype(BF16)
        k_sc[tile, head] = rotate(width + base).T.astype(BF16)
    v_sc[tile] = qkv[2 * width:3 * width].astype(BF16)
    m_sc[...] = jnp.full(m_sc.shape, NEG, F32)
    l_sc[...] = jnp.zeros(l_sc.shape, F32)
    acc_sc[...] = jnp.zeros(acc_sc.shape, F32)

    def block(key_tile, masked):
        if masked:
            key_index = key_tile * rows + lax.broadcasted_iota(jnp.int32, (rows, rows), 0)
            query_index = tile * rows + lax.broadcasted_iota(jnp.int32, (1, rows), 1)
            allowed = (key_index >= start_ref[...]) & (key_index <= query_index)
        for head in range(heads):
            scores = jnp.dot(k_sc[key_tile, head], q_sc[head], preferred_element_type=F32)
            if masked:
                scores = jnp.where(allowed, scores, NEG)
            old_max = m_sc[head]
            new_max = jnp.maximum(old_max, jnp.max(scores, axis=0, keepdims=True))
            prob = jnp.exp(scores - new_max)
            fade = jnp.exp(old_max - new_max)
            m_sc[head] = new_max
            l_sc[head] = fade * l_sc[head] + jnp.sum(prob, axis=0, keepdims=True)
            part = jnp.dot(v_sc[key_tile, head * head_dim:(head + 1) * head_dim], prob.astype(BF16), preferred_element_type=F32)
            acc_sc[head] = acc_sc[head] * fade + part

    def masked_step(key_tile, carry):
        block(key_tile, True)
        return carry

    def open_step(key_tile, carry):
        block(key_tile, False)
        return carry

    first_tile = bounds_ref[0, tile]
    open_tile = bounds_ref[1, tile]
    lax.fori_loop(first_tile, open_tile, masked_step, 0)
    lax.fori_loop(open_tile, tile, open_step, 0)
    block(tile, True)
    for head in range(heads):
        out_ref[0, head * head_dim:(head + 1) * head_dim] = (acc_sc[head] / l_sc[head]).astype(BF16)


def attention(normed, w_rows, cosines, sines, starts, parts, heads, head_dim, rows):
    seq_len, hidden = normed.shape
    tiles = seq_len // rows
    width = heads * head_dim
    per_part = tiles // parts
    first_start = starts[::rows]
    last_start = starts[rows - 1::rows]
    tile_index = jnp.arange(tiles, dtype=jnp.int32)
    bounds = jnp.stack([first_start // rows, jnp.minimum((last_start + rows - 1) // rows, tile_index)])
    grid_spec = pltpu.PrefetchScalarGridSpec(
        num_scalar_prefetch=1,
        grid=(tiles,),
        in_specs=[
            pl.BlockSpec((rows, hidden), lambda i, b: (i, 0)),
            pl.BlockSpec((3 * width, hidden), lambda i, b: (0, 0)),
            pl.BlockSpec((head_dim // 2, rows), lambda i, b: (0, i)),
            pl.BlockSpec((head_dim // 2, rows), lambda i, b: (0, i)),
            pl.BlockSpec((1, rows), lambda i, b: (0, i)),
        ],
        out_specs=pl.BlockSpec((1, width, rows), lambda i, b: (i // per_part, 0, i % per_part)),
        scratch_shapes=[
            pltpu.VMEM((heads, head_dim, rows), BF16),
            pltpu.VMEM((tiles, heads, rows, head_dim), BF16),
            pltpu.VMEM((tiles, width, rows), BF16),
            pltpu.VMEM((heads, 1, rows), F32),
            pltpu.VMEM((heads, 1, rows), F32),
            pltpu.VMEM((heads, head_dim, rows), F32),
        ],
    )
    flops = 2 * seq_len * hidden * 3 * width + 2 * seq_len * seq_len * width
    return pl.pallas_call(
        functools.partial(attention_kernel, heads, head_dim),
        grid_spec=grid_spec,
        out_shape=jax.ShapeDtypeStruct((parts, width, seq_len // parts), BF16),
        compiler_params=pltpu.CompilerParams(dimension_semantics=('arbitrary',), vmem_limit_bytes=VMEM_LIMIT),
        cost_estimate=pl.CostEstimate(flops=flops, bytes_accessed=4 * seq_len * hidden, transcendentals=seq_len * seq_len * heads // 2),
        name='attention',
    )(bounds, normed, w_rows, cosines, sines, starts[None, :])


def project_kernel(o_ref, w_ref, r_ref, gain_ref, res_ref, h_ref):
    parts = o_ref.shape[0]
    total = jnp.dot(w_ref[0], o_ref[0], preferred_element_type=F32)
    for part in range(1, parts):
        total = total + jnp.dot(w_ref[part], o_ref[part], preferred_element_type=F32)
    residual = r_ref[...].astype(F32) + total.T
    res_ref[...] = residual
    h_ref[...] = rms_norm(residual, gain_ref[...])


def project(heads_out, w_out, residual, gain, rows):
    parts, width, tokens = heads_out.shape
    hidden = residual.shape[1]
    return pl.pallas_call(
        project_kernel,
        grid=(tokens // rows,),
        in_specs=[
            pl.BlockSpec((parts, width, rows), lambda i: (0, 0, i)),
            pl.BlockSpec((parts, hidden, width), lambda i: (0, 0, 0)),
            pl.BlockSpec((rows, hidden), lambda i: (i, 0)),
            pl.BlockSpec((1, hidden), lambda i: (0, 0)),
        ],
        out_specs=[pl.BlockSpec((rows, hidden), lambda i: (i, 0)), pl.BlockSpec((rows, hidden), lambda i: (i, 0))],
        out_shape=[jax.ShapeDtypeStruct((tokens, hidden), F32), jax.ShapeDtypeStruct((tokens, hidden), BF16)],
        compiler_params=pltpu.CompilerParams(dimension_semantics=('arbitrary',), vmem_limit_bytes=VMEM_LIMIT),
        cost_estimate=pl.CostEstimate(flops=2 * tokens * hidden * parts * width, bytes_accessed=12 * tokens * hidden, transcendentals=0),
        name='project',
    )(heads_out, w_out, residual, gain)


def expert_kernel(tile_rows, h_ref, route_ref, gate_ref, up_ref, down_ref, out_ref):
    expert = pl.program_id(0)
    parts, part_rows, hidden = h_ref.shape
    shards, _, depth, width = gate_ref.shape
    gate_w = gate_ref[...].reshape(shards * depth, width)
    up_w = up_ref[...].reshape(shards * depth, width)
    down_w = down_ref[...].reshape(shards * depth, width)
    lanes = route_ref.shape[-1]
    lane_index = lax.broadcasted_iota(jnp.int32, (tile_rows, lanes), 1)
    group = tile_rows // part_rows
    for tile in range(parts // group):
        span = slice(tile * group, (tile + 1) * group)
        rows = h_ref[span].reshape(tile_rows, hidden)
        route = route_ref[span].reshape(tile_rows, lanes)
        share = jnp.sum(jnp.where(lane_index == expert, route, 0.0), axis=1, keepdims=True)
        gate_pre = jnp.dot(rows, gate_w, preferred_element_type=F32)
        up_pre = jnp.dot(rows, up_w, preferred_element_type=F32)
        act = (gate_pre * (1.0 / (1.0 + jnp.exp(-gate_pre))) * up_pre).astype(BF16)
        mixed = (share * lax.dot_general(act, down_w, NT, preferred_element_type=F32)).reshape(group, part_rows, hidden)

        @pl.when(expert == 0)
        def _():
            out_ref[span] = mixed

        @pl.when(expert > 0)
        def _():
            out_ref[span] += mixed


def expert_mix(normed, route, sub, gate_weight, up_weight, down_weight):
    parts, part_rows, hidden = normed.shape
    shards, num_experts, depth, width = gate_weight.shape
    lanes = route.shape[-1]
    tokens = parts * part_rows
    weight_spec = pl.BlockSpec((shards, 1, depth, width), lambda e: (0, e, 0, 0))
    return pl.pallas_call(
        functools.partial(expert_kernel, 2 * part_rows),
        grid=(num_experts,),
        in_specs=[
            pl.BlockSpec((parts, part_rows, hidden), lambda e: (0, 0, 0)),
            pl.BlockSpec((parts, None, part_rows, lanes), lambda e: (0, sub, 0, 0)),
            weight_spec,
            weight_spec,
            weight_spec,
        ],
        out_specs=pl.BlockSpec((parts, part_rows, hidden), lambda e: (0, 0, 0)),
        out_shape=jax.ShapeDtypeStruct((parts, part_rows, hidden), F32),
        compiler_params=pltpu.CompilerParams(dimension_semantics=('arbitrary',), vmem_limit_bytes=VMEM_LIMIT),
        cost_estimate=pl.CostEstimate(
            flops=6 * tokens * hidden * width * num_experts,
            bytes_accessed=6 * num_experts * hidden * width + 6 * tokens * hidden,
            transcendentals=tokens * width * num_experts,
        ),
        name='experts',
    )(normed, route, gate_weight, up_weight, down_weight)


def solution(mesh):
    token_spec = P(('rep', 'tok', 'mp'))
    row_spec = P(('rep', 'tok', 'mp'), None)
    head_weight = P(None, 'tok', 'mp', None)
    in_specs = (row_spec, token_spec, row_spec, row_spec, head_weight, head_weight, head_weight, P(None, 'mp', None, 'tok'), P(None, None, 'tok', 'mp'), P(None, None, 'tok', 'mp'), P(None, None, 'mp', 'tok'), P(None, None), P(None, None))
    parts = mesh.shape['mp']

    def device_step(hidden_in, seg_ids, expert_ids, expert_gates, w_query, w_key, w_value, w_out, w_gate, w_up, w_down, gain_attn, gain_mlp):
        num_layers, depth, heads, head_dim = w_query.shape
        tokens, hidden = hidden_in.shape
        seq_len = tokens * parts
        width = heads * head_dim
        subs = 4
        sub_rows = tokens // subs

        qkv_local = jnp.concatenate([w[layer].reshape(depth, width) for layer in range(num_layers) for w in (w_query, w_key, w_value)], axis=1)
        qkv_all = lax.all_gather(qkv_local, 'tok', axis=0, tiled=True)
        out_local = jnp.concatenate([w_out[layer].reshape(width, depth).T for layer in range(num_layers)], axis=1)
        out_all = lax.all_gather(out_local, ('mp', 'tok'), axis=0, tiled=True).reshape(parts, hidden, num_layers * width)
        ints = lax.all_gather(jnp.concatenate([seg_ids[:, None], expert_ids], axis=1).T, 'mp', axis=0)
        gates = lax.all_gather(expert_gates.T, 'mp', axis=0)
        starts = request_starts(ints[:, 0].reshape(seq_len))
        positions = (jnp.arange(seq_len, dtype=jnp.int32) - starts).astype(F32)
        inv_freq = jnp.power(ROPE_BASE, -jnp.arange(head_dim // 2, dtype=F32) * 2.0 / head_dim)
        angles = inv_freq[:, None] * positions[None, :]
        cosines = jnp.cos(angles)
        sines = jnp.sin(angles)
        expert_lane = jnp.arange(128, dtype=jnp.int32)
        route = jnp.zeros((parts, tokens, 128), F32)
        for choice in range(expert_ids.shape[1]):
            route = route + jnp.where(ints[:, 1 + choice][..., None] == expert_lane, gates[:, choice][..., None], 0.0)
        route = route.reshape(parts, subs, sub_rows, 128)

        residual = hidden_in.astype(F32)
        for layer in range(num_layers):
            gate_weight = lax.all_gather(w_gate[layer], 'tok', axis=0)
            up_weight = lax.all_gather(w_up[layer], 'tok', axis=0)
            down_weight = lax.all_gather(jnp.swapaxes(w_down[layer], 1, 2), 'tok', axis=0)
            w_rows = qkv_all[:, layer * 3 * width:(layer + 1) * 3 * width].T
            o_weight = out_all[:, :, layer * width:(layer + 1) * width]
            normed = lax.all_gather(rms_norm(residual, gain_attn[layer]), 'mp', axis=0, tiled=True)
            heads_out = attention(normed, w_rows, cosines, sines, starts, parts, heads, head_dim, min(512, tokens))
            heads_out = lax.all_to_all(heads_out, 'mp', 0, 0)
            residual, normed = project(heads_out, o_weight, residual, gain_mlp[layer][None, :], min(256, tokens))
            sums = []
            for sub in range(subs):
                rows = slice(sub * sub_rows, (sub + 1) * sub_rows)
                sub_normed = lax.all_gather(normed[rows], 'mp', axis=0)
                mixed = expert_mix(sub_normed, route, sub, gate_weight, up_weight, down_weight)
                sums.append(residual[rows] + lax.psum_scatter(mixed.reshape(parts * sub_rows, hidden), 'mp', scatter_dimension=0, tiled=True))
            residual = jnp.concatenate(sums, axis=0)
        return residual

    return jax.shard_map(device_step, mesh=mesh, in_specs=in_specs, out_specs=row_spec, check_vma=False)
```

time: 2130 us -> 1100 us (0.52)
  other arithmetic: 502 us -> 24.3 us
  matrix products: 412 us -> 0 us
  Pallas kernels: 238 us -> 444 us
  local copies, waits for them, and re-layouts: 207 us -> 27.7 us
  blocking collectives: 211 us -> 42 us
    pallas_call x0 -> x12, Pallas kernels: none -> 444 us  [the longest x8 340 us: expert_mix(): pl.pallas_call(functools.partial(expert_kernel, 2 * part_rows), grid=(num...]
    dot_general x34 -> x0, matrix products: 393 us -> none  [the longest x16 193 us: one_block(): jnp.einsum('hgbs,shd->bhgd', attn_prob, v_all, preferred_element_type=jnp...]
    reduce_scatter x4 -> x8, waiting for transfers between devices: 454 us -> 113 us  [device_step(): lax.psum_scatter(mixed.reshape(parts * sub_rows, hidden), 'mp', scatter_d...]
    another operation x6 -> x0, Pallas kernels: 237 us -> none
    all_gather x8 -> x16, waiting for transfers between devices: 75.9 us -> 288 us  [the longest x2 107 us: device_step(): lax.all_gather(jnp.swapaxes(w_down[layer], 1, 2), 'tok', axis=0)]
    reduce_sum x16 -> x0, other arithmetic: 191 us -> none  [one_block(): jax.nn.softmax(jnp.where(allowed, scores, -1e+30), axis=-1)]
    all_gather x11 -> x2, blocking collectives: 211 us -> 21.4 us  [the longest x1 12.3 us: device_step(): lax.all_gather(jnp.concatenate([seg_ids[:, None], expert_ids], axis=1).T,...]
    scatter-add x3 -> x0, other arithmetic: 184 us -> none  [the longest x2 127 us: expert_mix(): jax.ops.segment_sum(down_out * pair_gate[:, None], pair_token, num_segmen...]
  transfers between devices with their start and end apart: 14 -> 27, of which waited for: 7 -> 15; matrix products, arithmetic and copies ran while one was open for 12% -> 3% of each run, Pallas kernels for 4% -> 40%
where the time goes in v1:
time: 1100 us; the launch traced here: 1090 us
  waiting for transfers between devices  535 us (49%)
  Pallas kernels  444 us (40%)
  blocking collectives  42 us (4%)
  local copies, waits for them, and re-layouts  27.7 us (3%)
  other arithmetic  24.3 us (2%)
  between operations  14.1 us (1%)
    pallas_call x8, Pallas kernels, expert_mix(): pl.pallas_call(functools.partial(expert_kernel, 2 * part_rows), grid=(num...  340 us
    all_gather x2, waiting for transfers between devices, device_step(): lax.all_gather(rms_norm(residual, gain_attn[layer]), 'mp', axis=0, tiled=...  119 us
    reduce_scatter x8, waiting for transfers between devices, device_step(): lax.psum_scatter(mixed.reshape(parts * sub_rows, hidden), 'mp', scatter_d...  113 us
    all_gather x2, waiting for transfers between devices, device_step(): lax.all_gather(jnp.swapaxes(w_down[layer], 1, 2), 'tok', axis=0)  107 us
    pallas_call x2, Pallas kernels, attention(): pl.pallas_call(functools.partial(attention_kernel, heads, head_dim), grid...  90.5 us
    all_gather x2, waiting for transfers between devices, device_step(): up_weight = lax.all_gather(w_up[layer], 'tok', axis=0)  83.1 us
    all_gather x2, waiting for transfers between devices, device_step(): gate_weight = lax.all_gather(w_gate[layer], 'tok', axis=0)  53.5 us
    all_gather x8, waiting for transfers between devices, device_step(): sub_normed = lax.all_gather(normed[rows], 'mp', axis=0)  39.4 us
  transfers between devices with their start and end apart: 27, of which 15 were waited for; matrix products, arithmetic and copies ran while one was open for 3% of the time, Pallas kernels for 40%

profile of v1, /device:TPU:97, one launch (start us, length us, event | category | flops | bytes accessed | tf_op | source)
XLA Modules:
  0.0 1093.5 jit_solution(16471847303326683245)
XLA Ops:
  41.1 60.2 %all-gather.33.cloned.1.call-done.h_ref = bf16[4096,768]{1,0:T(8,128)(2,1)} async-done(((bf16[1024,768]{1,0:T(8,128)(2,1)}), bf16[4096,768]{1,0:T(8,128)(2,1)}) %all-gather.33.cloned.1.call-update) | async-done | bytes 6291472 | tf_op jit(solution)/shard_map/all_gather | solution.py:257
  101.3 45.2 %attention.2 = bf16[4,192,1024]{2,1,0:T(8,128)(2,1)} custom-call(s32[2,8]{1,0:T(2,128)} %pad_add_fusion.bounds_ref, bf16[4096,768]{1,0:T(8,128)(2,1)} %all-gather.33.cloned.1.call-done.h_ref, bf16[576,768]{1,0:T(8,128)(2,1)} %bitcast.69, f32[32,4096]{1,0:T(8,128)} %get-tuple-element.59.cos_ref, f32[32,4096]{1,0:T(8,128)} %get-tuple-element.58.sin_ref, ...), custom_call_target="tpu_custom_call" | custom-call | flops 10066329600 | bytes 12582912 | tf_op jit(solution)/shard_map/attention/pallas_call | solution.py:120
  199.2 14.1 %all-gather.49.cloned.1.call-done = bf16[1024,768]{1,0:T(8,128)(2,1)} async-done(((bf16[256,768]{1,0:T(8,128)(2,1)}), bf16[1024,768]{1,0:T(8,128)(2,1)}) %all-gather.49.cloned.1.call-update) | async-done | bytes 1572880 | tf_op jit(solution)/shard_map/all_gather | solution.py:264
  213.3 53.5 %all-gather.39.cloned.1.call-done.gate_ref = bf16[8,8,96,768]{3,2,1,0:T(8,128)(2,1)} async-done(((bf16[1,8,96,768]{3,2,1,0:T(8,128)(2,1)}), bf16[8,8,96,768]{3,2,1,0:T(8,128)(2,1)}) %all-gather.39.cloned.1.call-update) | async-done | bytes 9437200 | tf_op jit(solution)/shard_map/all_gather | solution.py:252
  266.8 53.2 %all-gather.41.cloned.1.call-done.up_ref = bf16[8,8,96,768]{3,2,1,0:T(8,128)(2,1)} async-done(((bf16[1,8,96,768]{3,2,1,0:T(8,128)(2,1)}), bf16[8,8,96,768]{3,2,1,0:T(8,128)(2,1)}) %all-gather.41.cloned.1.call-update) | async-done | bytes 9437200 | tf_op jit(solution)/shard_map/all_gather | solution.py:253
  320.0 53.3 %all-gather.51.cloned.1.call-done = bf16[64,96,768]{2,1,0:T(8,128)(2,1)} async-done(((bf16[8,96,768]{2,1,0:T(8,128)(2,1)}), bf16[64,96,768]{2,1,0:T(8,128)(2,1)}) %all-gather.51.cloned.1.call-update) | async-done | bytes 9437200 | tf_op jit(solution)/shard_map/all_gather | solution.py:254
  373.3 42.5 %experts.8 = f32[4,256,768]{2,1,0:T(8,128)} custom-call(bf16[4,256,768]{2,1,0:T(8,128)(2,1)} %bitcast.95, f32[4,4,256,128]{3,2,1,0:T(8,128)} %select_add_fusion.route_ref, bf16[8,8,96,768]{3,2,1,0:T(8,128)(2,1)} %all-gather.39.cloned.1.call-done.gate_ref, bf16[8,8,96,768]{3,2,1,0:T(8,128)(2,1)} %all-gather.41.cloned.1.call-done.up_ref, ...), custom_call_target="tpu_custom_call" | custom-call | flops 28991029248 | bytes 33030144 | tf_op jit(solution)/shard_map/experts/pallas_call | solution.py:195
  415.9 42.5 %experts.11 = f32[4,256,768]{2,1,0:T(8,128)} custom-call(bf16[4,256,768]{2,1,0:T(8,128)(2,1)} %bitcast.97, f32[4,4,256,128]{3,2,1,0:T(8,128)} %select_add_fusion.route_ref, bf16[8,8,96,768]{3,2,1,0:T(8,128)(2,1)} %all-gather.39.cloned.1.call-done.gate_ref, bf16[8,8,96,768]{3,2,1,0:T(8,128)(2,1)} %all-gather.41.cloned.1.call-done.up_ref, ...), custom_call_target="tpu_custom_call" | custom-call | flops 28991029248 | bytes 33030144 | tf_op jit(solution)/shard_map/experts/pallas_call | solution.py:195
  458.8 42.5 %experts.10 = f32[4,256,768]{2,1,0:T(8,128)} custom-call(bf16[4,256,768]{2,1,0:T(8,128)(2,1)} %bitcast.96, f32[4,4,256,128]{3,2,1,0:T(8,128)} %select_add_fusion.route_ref, bf16[8,8,96,768]{3,2,1,0:T(8,128)(2,1)} %all-gather.39.cloned.1.call-done.gate_ref, bf16[8,8,96,768]{3,2,1,0:T(8,128)(2,1)} %all-gather.41.cloned.1.call-done.up_ref, ...), custom_call_target="tpu_custom_call" | custom-call | flops 28991029248 | bytes 33030144 | tf_op jit(solution)/shard_map/experts/pallas_call | solution.py:195
  501.5 42.5 %experts.9 = f32[4,256,768]{2,1,0:T(8,128)} custom-call(bf16[4,256,768]{2,1,0:T(8,128)(2,1)} %bitcast.99, f32[4,4,256,128]{3,2,1,0:T(8,128)} %select_add_fusion.route_ref, bf16[8,8,96,768]{3,2,1,0:T(8,128)(2,1)} %all-gather.39.cloned.1.call-done.gate_ref, bf16[8,8,96,768]{3,2,1,0:T(8,128)(2,1)} %all-gather.41.cloned.1.call-done.up_ref, ...), custom_call_target="tpu_custom_call" | custom-call | flops 28991029248 | bytes 33030144 | tf_op jit(solution)/shard_map/experts/pallas_call | solution.py:195
  544.2 18.8 %reduce-scatter.13.cloned.1.call-done = f32[256,768]{1,0:T(8,128)} async-done(((f32[1024,768]{1,0:T(8,128)}), f32[256,768]{1,0:T(8,128)}) %reduce-scatter.13.cloned.1.call-update) | async-done | bytes 786448 | tf_op jit(solution)/shard_map/reduce_scatter | solution.py:266
  563.0 37.7 %reduce-scatter.11.cloned.1.call-done = f32[256,768]{1,0:T(8,128)} async-done(((f32[1024,768]{1,0:T(8,128)}), f32[256,768]{1,0:T(8,128)}) %reduce-scatter.11.cloned.1.call-update) | async-done | bytes 786448 | tf_op jit(solution)/shard_map/reduce_scatter | solution.py:266
  610.1 59.1 %all-gather.43.cloned.1.call-done.h_ref = bf16[4096,768]{1,0:T(8,128)(2,1)} async-done(((bf16[1024,768]{1,0:T(8,128)(2,1)}), bf16[4096,768]{1,0:T(8,128)(2,1)}) %all-gather.43.cloned.1.call-update) | async-done | bytes 6291472 | tf_op jit(solution)/shard_map/all_gather | solution.py:257
  669.3 45.2 %attention.3 = bf16[4,192,1024]{2,1,0:T(8,128)(2,1)} custom-call(s32[2,8]{1,0:T(2,128)} %pad_add_fusion.bounds_ref, bf16[4096,768]{1,0:T(8,128)(2,1)} %all-gather.43.cloned.1.call-done.h_ref, bf16[576,768]{1,0:T(8,128)(2,1)} %bitcast.68, f32[32,4096]{1,0:T(8,128)} %get-tuple-element.59.cos_ref, f32[32,4096]{1,0:T(8,128)} %get-tuple-element.58.sin_ref, ...), custom_call_target="tpu_custom_call" | custom-call | flops 10066329600 | bytes 12582912 | tf_op jit(solution)/shard_map/attention/pallas_call | solution.py:120
  714.5 20.6 %all_to_all.10.o_ref = bf16[4,192,1024]{2,1,0:T(8,128)(2,1)} all-to-all(bf16[4,192,1024]{2,1,0:T(8,128)(2,1)} %attention.3), channel_id=1, replica_groups=mesh['rep'=1,'mp'=4,'tok'=8] {'mp'}, dimensions={0} | all-to-all | bytes 3145728 | tf_op jit(solution)/shard_map/all_to_all | solution.py:259
  746.7 29.9 %all-gather.47.cloned.1.call-done.up_ref = bf16[8,8,96,768]{3,2,1,0:T(8,128)(2,1)} async-done(((bf16[1,8,96,768]{3,2,1,0:T(8,128)(2,1)}), bf16[8,8,96,768]{3,2,1,0:T(8,128)(2,1)}) %all-gather.47.cloned.1.call-update) | async-done | bytes 9437200 | tf_op jit(solution)/shard_map/all_gather | solution.py:253
  776.6 53.2 %all-gather.61.cloned.1.call-done = bf16[64,96,768]{2,1,0:T(8,128)(2,1)} async-done(((bf16[8,96,768]{2,1,0:T(8,128)(2,1)}), bf16[64,96,768]{2,1,0:T(8,128)(2,1)}) %all-gather.61.cloned.1.call-update) | async-done | bytes 9437200 | tf_op jit(solution)/shard_map/all_gather | solution.py:254
  829.8 25.2 %all-gather.59.cloned.1.call-done = bf16[1024,768]{1,0:T(8,128)(2,1)} async-done(((bf16[256,768]{1,0:T(8,128)(2,1)}), bf16[1024,768]{1,0:T(8,128)(2,1)}) %all-gather.59.cloned.1.call-update) | async-done | bytes 1572880 | tf_op jit(solution)/shard_map/all_gather | solution.py:264
  855.0 42.5 %experts.12 = f32[4,256,768]{2,1,0:T(8,128)} custom-call(bf16[4,256,768]{2,1,0:T(8,128)(2,1)} %bitcast.102, f32[4,4,256,128]{3,2,1,0:T(8,128)} %select_add_fusion.route_ref, bf16[8,8,96,768]{3,2,1,0:T(8,128)(2,1)} %all-gather.45.cloned.1.call-done.gate_ref, bf16[8,8,96,768]{3,2,1,0:T(8,128)(2,1)} %all-gather.47.cloned.1.call-done.up_ref, ...), custom_call_target="tpu_custom_call" | custom-call | flops 28991029248 | bytes 33030144 | tf_op jit(solution)/shard_map/experts/pallas_call | solution.py:195
  897.8 42.5 %experts.15 = f32[4,256,768]{2,1,0:T(8,128)} custom-call(bf16[4,256,768]{2,1,0:T(8,128)(2,1)} %bitcast.101, f32[4,4,256,128]{3,2,1,0:T(8,128)} %select_add_fusion.route_ref, bf16[8,8,96,768]{3,2,1,0:T(8,128)(2,1)} %all-gather.45.cloned.1.call-done.gate_ref, bf16[8,8,96,768]{3,2,1,0:T(8,128)(2,1)} %all-gather.47.cloned.1.call-done.up_ref, ...), custom_call_target="tpu_custom_call" | custom-call | flops 28991029248 | bytes 33030144 | tf_op jit(solution)/shard_map/experts/pallas_call | solution.py:195
  940.5 42.6 %experts.14 = f32[4,256,768]{2,1,0:T(8,128)} custom-call(bf16[4,256,768]{2,1,0:T(8,128)(2,1)} %bitcast.100, f32[4,4,256,128]{3,2,1,0:T(8,128)} %select_add_fusion.route_ref, bf16[8,8,96,768]{3,2,1,0:T(8,128)(2,1)} %all-gather.45.cloned.1.call-done.gate_ref, bf16[8,8,96,768]{3,2,1,0:T(8,128)(2,1)} %all-gather.47.cloned.1.call-done.up_ref, ...), custom_call_target="tpu_custom_call" | custom-call | flops 28991029248 | bytes 33030144 | tf_op jit(solution)/shard_map/experts/pallas_call | solution.py:195
  983.5 42.5 %experts.13 = f32[4,256,768]{2,1,0:T(8,128)} custom-call(bf16[4,256,768]{2,1,0:T(8,128)(2,1)} %bitcast.98, f32[4,4,256,128]{3,2,1,0:T(8,128)} %select_add_fusion.route_ref, bf16[8,8,96,768]{3,2,1,0:T(8,128)(2,1)} %all-gather.45.cloned.1.call-done.gate_ref, bf16[8,8,96,768]{3,2,1,0:T(8,128)(2,1)} %all-gather.47.cloned.1.call-done.up_ref, ...), custom_call_target="tpu_custom_call" | custom-call | flops 28991029248 | bytes 33030144 | tf_op jit(solution)/shard_map/experts/pallas_call | solution.py:195
  1026.1 18.9 %reduce-scatter.21.cloned.1.call-done = f32[256,768]{1,0:T(8,128)} async-done(((f32[1024,768]{1,0:T(8,128)}), f32[256,768]{1,0:T(8,128)}) %reduce-scatter.21.cloned.1.call-update) | async-done | bytes 786448 | tf_op jit(solution)/shard_map/reduce_scatter | solution.py:266
  1045.0 37.7 %reduce-scatter.19.cloned.1.call-done = f32[256,768]{1,0:T(8,128)} async-done(((f32[1024,768]{1,0:T(8,128)}), f32[256,768]{1,0:T(8,128)}) %reduce-scatter.19.cloned.1.call-update) | async-done | bytes 786448 | tf_op jit(solution)/shard_map/reduce_scatter | solution.py:266
  (155 shorter events, 113.6 us)
Async XLA Ops:
  10.2 91.1 %all-gather.33.cloned.1.call-start = ((), (), s32[]{:S(2)}) async-start(), calls=%async_computation.10 | async-start | bytes 7864320 | tf_op jit(solution)/shard_map/all_gather | solution.py:257
  13.7 139.1 %all-gather.37.cloned.1.call-start = ((), (), s32[]{:S(2)}) async-start(), calls=%async_computation.12 | async-start | bytes 2433024 | tf_op jit(solution)/shard_map/all_gather | solution.py:235
  176.5 90.3 %all-gather.39.cloned.1.call-start = ((), (), s32[]{:S(2)}) async-start(), calls=%async_computation.13 | async-start | bytes 10616832 | tf_op jit(solution)/shard_map/all_gather | solution.py:252
  178.2 141.8 %all-gather.41.cloned.1.call-start = ((), (), s32[]{:S(2)}) async-start(), calls=%async_computation.14 | async-start | bytes 10616832 | tf_op jit(solution)/shard_map/all_gather | solution.py:253
  181.8 191.5 %all-gather.51.cloned.1.call-start = ((), (), s32[]{:S(2)}) async-start(), calls=%async_computation.27 | async-start | bytes 10616832 | tf_op jit(solution)/shard_map/all_gather | solution.py:254
  183.5 232.4 %all-gather.57.cloned.1.call-start = ((), (), s32[]{:S(2)}) async-start(), calls=%async_computation.30 | async-start | bytes 1966080 | tf_op jit(solution)/shard_map/all_gather | solution.py:264
  184.4 274.5 %all-gather.55.cloned.1.call-start = ((), (), s32[]{:S(2)}) async-start(), calls=%async_computation.29 | async-start | bytes 1966080 | tf_op jit(solution)/shard_map/all_gather | solution.py:264
  185.1 316.4 %all-gather.53.cloned.1.call-start = ((), (), s32[]{:S(2)}) async-start(), calls=%async_computation.28 | async-start | bytes 1966080 | tf_op jit(solution)/shard_map/all_gather | solution.py:264
  199.2 345.0 %reduce-scatter.9.cloned.1.call-start = ((), (), s32[]{:S(2)}) async-start(), calls=%async_computation.15 | async-start | bytes 3932160 | tf_op jit(solution)/shard_map/reduce_scatter | solution.py:266
  415.8 128.4 %reduce-scatter.15.cloned.1.call-start = ((), (), s32[]{:S(2)}) async-start(), calls=%async_computation.18 | async-start | bytes 3932160 | tf_op jit(solution)/shard_map/reduce_scatter | solution.py:266
  458.5 104.5 %reduce-scatter.13.cloned.1.call-start = ((), (), s32[]{:S(2)}) async-start(), calls=%async_computation.17 | async-start | bytes 3932160 | tf_op jit(solution)/shard_map/reduce_scatter | solution.py:266
  501.4 99.2 %reduce-scatter.11.cloned.1.call-start = ((), (), s32[]{:S(2)}) async-start(), calls=%async_computation.16 | async-start | bytes 3932160 | tf_op jit(solution)/shard_map/reduce_scatter | solution.py:266
  544.1 125.2 %all-gather.43.cloned.1.call-start = ((), (), s32[]{:S(2)}) async-start(), calls=%async_computation.19 | async-start | bytes 7864320 | tf_op jit(solution)/shard_map/all_gather | solution.py:257
  606.4 140.3 %all-gather.45.cloned.1.call-start = ((), (), s32[]{:S(2)}) async-start(), calls=%async_computation.20 | async-start | bytes 10616832 | tf_op jit(solution)/shard_map/all_gather | solution.py:252
  607.0 169.6 %all-gather.47.cloned.1.call-start = ((), (), s32[]{:S(2)}) async-start(), calls=%async_computation.21 | async-start | bytes 10616832 | tf_op jit(solution)/shard_map/all_gather | solution.py:253
  607.7 222.1 %all-gather.61.cloned.1.call-start = ((), (), s32[]{:S(2)}) async-start(), calls=%async_computation.32 | async-start | bytes 10616832 | tf_op jit(solution)/shard_map/all_gather | solution.py:254
  608.3 246.7 %all-gather.59.cloned.1.call-start = ((), (), s32[]{:S(2)}) async-start(), calls=%async_computation.31 | async-start | bytes 1966080 | tf_op jit(solution)/shard_map/all_gather | solution.py:264
  744.4 153.4 %all-gather.67.cloned.1.call-start = ((), (), s32[]{:S(2)}) async-start(), calls=%async_computation.35 | async-start | bytes 1966080 | tf_op jit(solution)/shard_map/all_gather | solution.py:264
  745.0 195.5 %all-gather.65.cloned.1.call-start = ((), (), s32[]{:S(2)}) async-start(), calls=%async_computation.34 | async-start | bytes 1966080 | tf_op jit(solution)/shard_map/all_gather | solution.py:264
  745.8 237.6 %all-gather.63.cloned.1.call-start = ((), (), s32[]{:S(2)}) async-start(), calls=%async_computation.33 | async-start | bytes 1966080 | tf_op jit(solution)/shard_map/all_gather | solution.py:264
  746.6 279.4 %reduce-scatter.17.cloned.1.call-start = ((), (), s32[]{:S(2)}) async-start(), calls=%async_computation.22 | async-start | bytes 3932160 | tf_op jit(solution)/shard_map/reduce_scatter | solution.py:266
  897.5 128.5 %reduce-scatter.23.cloned.1.call-start = ((), (), s32[]{:S(2)}) async-start(), calls=%async_computation.25 | async-start | bytes 3932160 | tf_op jit(solution)/shard_map/reduce_scatter | solution.py:266
  940.4 104.6 %reduce-scatter.21.cloned.1.call-start = ((), (), s32[]{:S(2)}) async-start(), calls=%async_computation.24 | async-start | bytes 3932160 | tf_op jit(solution)/shard_map/reduce_scatter | solution.py:266
  983.1 99.5 %reduce-scatter.19.cloned.1.call-start = ((), (), s32[]{:S(2)}) async-start(), calls=%async_computation.23 | async-start | bytes 3932160 | tf_op jit(solution)/shard_map/reduce_scatter | solution.py:266
  (17 other events, 267.7 us)
Sparse Core Ops, SparseCore 0:
  10.3 26.4 all-gather.34
  38.4 62.8 all-gather.32
  103.4 39.9 all-gather.36
  176.6 36.6 all-gather.48
  214.7 51.9 all-gather.38
  268.2 51.7 all-gather.40
  321.5 51.7 all-gather.50
  400.1 23.8 all-gather.54
  425.4 23.8 all-gather.52
  451.7 35.8 reduce-scatter.8
  489.7 35.4 reduce-scatter.14
  527.5 35.4 reduce-scatter.12
  565.2 35.4 reduce-scatter.10
  606.5 62.6 all-gather.42
  670.7 52.6 all-gather.44
  724.8 51.7 all-gather.46
  778.0 51.7 all-gather.60
  856.4 23.8 all-gather.66
  881.9 23.8 all-gather.64
  907.4 23.8 all-gather.62
  933.7 35.8 reduce-scatter.16
  971.7 35.4 reduce-scatter.22
  1009.5 35.4 reduce-scatter.20
  1047.1 35.4 reduce-scatter.18
  (2 shorter events, 47.1 us)

commit v2 on v1

v2 whole, which is shorter than its diff:
```python
import functools

import jax
import jax.numpy as jnp
from jax import lax
from jax.experimental import pallas as pl
from jax.experimental.pallas import tpu as pltpu
from jax.sharding import PartitionSpec as P

EPS = 1e-5
ROPE_BASE = 10000.0
NEG = -1e30
VMEM_LIMIT = 63 * 1024 * 1024
F32 = jnp.float32
BF16 = jnp.bfloat16
NT = (((1,), (1,)), ((), ()))
MESH = pl.DeviceIdType.MESH


def rms_norm(residual, gain):
    inv_rms = lax.rsqrt(jnp.mean(residual * residual, axis=-1, keepdims=True) + EPS)
    return (residual * inv_rms * gain.astype(F32)).astype(BF16)


def request_starts(seg_rows):
    token_index = jnp.arange(seg_rows.shape[0], dtype=jnp.int32)
    is_start = jnp.concatenate([jnp.ones((1,), dtype=jnp.bool_), seg_rows[1:] != seg_rows[:-1]])
    return lax.cummax(jnp.where(is_start, token_index, 0), axis=0)


class Wire:
    def __init__(self, send_sem, recv_sem):
        self.send_sem = send_sem
        self.recv_sem = recv_sem

    def copy(self, slot, src, dst, device):
        return pltpu.make_async_remote_copy(src_ref=src, dst_ref=dst, send_sem=self.send_sem.at[slot], recv_sem=self.recv_sem.at[slot], device_id=device, device_id_type=MESH)


def ring(axis, size):
    me = lax.axis_index(axis)
    return me, lax.rem(me + size - 1, size), lax.rem(me + 1, size), lax.rem(me + size // 2, size)


def meet(devices):
    barrier = pltpu.get_barrier_semaphore()
    for device in devices:
        pl.semaphore_signal(barrier, inc=1, device_id=device, device_id_type=MESH)
    pl.semaphore_wait(barrier, len(devices))


def row_gather(wire, base, own, rows_all, left, right, me):
    half = own.shape[0] // 2
    low, high = pl.ds(0, half), pl.ds(half, half)
    to_right, to_left = {'mp': right}, {'mp': left}
    return {
        'right_low': wire.copy(base, own.at[low], rows_all.at[me, low], to_right),
        'right_high': wire.copy(base + 1, own.at[high], rows_all.at[me, high], to_right),
        'left_high': wire.copy(base + 2, own.at[high], rows_all.at[me, high], to_left),
        'left_low': wire.copy(base + 3, own.at[low], rows_all.at[me, low], to_left),
        'on_right': wire.copy(base + 4, rows_all.at[left, low], rows_all.at[left, low], to_right),
        'on_left': wire.copy(base + 5, rows_all.at[right, high], rows_all.at[right, high], to_left),
    }


FIRST = ('right_low', 'left_high', 'right_high', 'left_low')


def gather_kernel(parts, shards, hidden_ref, gain_ref, ints_ref, gates_ref, qkv_ref, out_ref, rows_all, ints_all, gates_all, qkv_all, out_all, own, send_sem, recv_sem, local_sem):
    me, left, right, _ = ring('mp', parts)
    tok = lax.axis_index('tok')
    partner = tok + 1 - 2 * lax.rem(tok, 2)
    strides = [2 * step for step in range(1, shards // 2)]
    peers = [{'tok': lax.rem(tok + stride, shards)} for stride in strides]
    to_left, to_right, to_partner = {'mp': left}, {'mp': right}, {'tok': partner}
    meet([to_left, to_right, to_partner] + peers)
    wire = Wire(send_sem, recv_sem)
    small = [
        wire.copy(0, out_ref, out_all.at[tok, me], to_right),
        wire.copy(1, out_ref, out_all.at[tok, me], to_left),
        wire.copy(2, ints_ref, ints_all.at[me], to_right),
        wire.copy(3, ints_ref, ints_all.at[me], to_left),
        wire.copy(4, gates_ref, gates_all.at[me], to_right),
        wire.copy(5, gates_ref, gates_all.at[me], to_left),
    ]
    local = [
        pltpu.make_async_copy(out_ref, out_all.at[tok, me], local_sem.at[0]),
        pltpu.make_async_copy(ints_ref, ints_all.at[me], local_sem.at[1]),
        pltpu.make_async_copy(gates_ref, gates_all.at[me], local_sem.at[2]),
        pltpu.make_async_copy(qkv_ref, qkv_all.at[tok], local_sem.at[3]),
    ]
    slot = 6
    qkv_out = []
    for peer in peers:
        qkv_out.append(wire.copy(slot, qkv_ref, qkv_all.at[tok], peer))
        slot += 1
    qkv_cross = [wire.copy(slot, qkv_ref, qkv_all.at[tok], to_partner)]
    slot += 1
    for stride in strides:
        source = lax.rem(tok + shards - stride, shards)
        qkv_cross.append(wire.copy(slot, qkv_all.at[source], qkv_all.at[source], to_partner))
        slot += 1
    for copy in small + local + qkv_out + qkv_cross[:1]:
        copy.start()
    own[...] = rms_norm(hidden_ref[...].astype(F32), gain_ref[...])
    rows = row_gather(wire, slot, own, rows_all, left, right, me)
    slot += 6
    rows_local = pltpu.make_async_copy(own, rows_all.at[me], local_sem.at[4])
    for name in FIRST:
        rows[name].start()
    rows_local.start()
    onward = [
        wire.copy(slot, out_all.at[tok, left], out_all.at[tok, left], to_right),
        wire.copy(slot + 1, ints_all.at[left], ints_all.at[left], to_right),
        wire.copy(slot + 2, gates_all.at[right], gates_all.at[right], to_left),
    ]
    slot += 3
    for copy in small:
        copy.wait_recv()
    for copy in onward:
        copy.start()
    for copy, after in zip(qkv_cross[1:], qkv_out):
        after.wait_recv()
        copy.start()
    onward[0].wait_recv()
    local[0].wait()
    out_out = []
    for peer in peers:
        out_out.append(wire.copy(slot, out_all.at[tok], out_all.at[tok], peer))
        slot += 1
    out_cross = [wire.copy(slot, out_all.at[tok], out_all.at[tok], to_partner)]
    slot += 1
    for stride in strides:
        source = lax.rem(tok + shards - stride, shards)
        out_cross.append(wire.copy(slot, out_all.at[source], out_all.at[source], to_partner))
        slot += 1
    for copy in out_out + out_cross[:1]:
        copy.start()
    for copy, after in zip(out_cross[1:], out_out):
        after.wait_recv()
        copy.start()
    rows['right_low'].wait_recv()
    rows['on_right'].start()
    rows['left_high'].wait_recv()
    rows['on_left'].start()
    for copy in onward[1:] + qkv_cross + out_cross:
        copy.wait_recv()
    for name in ('right_high', 'left_low', 'on_right', 'on_left'):
        rows[name].wait_recv()
    for copy in small + onward + qkv_out + qkv_cross + out_out + out_cross + list(rows.values()):
        copy.wait_send()
    for copy in local[1:] + [rows_local]:
        copy.wait()


def gather_start(hidden_in, gain, ints, gates, qkv_local, out_local, parts, shards):
    tokens, hidden = hidden_in.shape
    copies = 6 + 2 * (shards - 2) // 2 + 1 + 6 + 3 + 2 * (shards - 2) // 2 + 1
    anywhere = pl.BlockSpec(memory_space=pl.ANY)
    vmem = pl.BlockSpec(memory_space=pltpu.VMEM)
    return pl.pallas_call(
        functools.partial(gather_kernel, parts, shards),
        in_specs=[vmem, vmem, vmem, vmem, vmem, vmem],
        out_specs=[anywhere] * 5,
        out_shape=[
            jax.ShapeDtypeStruct((parts, tokens, hidden), BF16),
            jax.ShapeDtypeStruct((parts,) + ints.shape, jnp.int32),
            jax.ShapeDtypeStruct((parts,) + gates.shape, F32),
            jax.ShapeDtypeStruct((shards,) + qkv_local.shape, BF16),
            jax.ShapeDtypeStruct((shards, parts) + out_local.shape, BF16),
        ],
        scratch_shapes=[
            pltpu.VMEM((tokens, hidden), BF16),
            pltpu.SemaphoreType.DMA((copies,)),
            pltpu.SemaphoreType.DMA((copies,)),
            pltpu.SemaphoreType.DMA((5,)),
        ],
        compiler_params=pltpu.CompilerParams(collective_id=0, has_side_effects=True, vmem_limit_bytes=VMEM_LIMIT),
        cost_estimate=pl.CostEstimate(flops=20_000_000_000, bytes_accessed=2 * parts * tokens * hidden, transcendentals=0),
        name='gather_start',
    )(hidden_in, gain, ints, gates, qkv_local, out_local)


def attention_kernel(heads, head_dim, bounds_ref, h_ref, w_ref, cos_ref, sin_ref, start_ref, out_ref, w_sc, q_sc, k_sc, v_sc, m_sc, l_sc, acc_sc):
    tile = pl.program_id(0)
    rows = h_ref.shape[0]
    width = heads * head_dim
    half = head_dim // 2

    @pl.when(tile == 0)
    def _():
        w_sc[...] = w_ref[:, 0].reshape(w_sc.shape[1], 3 * width).astype(F32).T.astype(BF16)

    qkv = lax.dot_general(w_sc[...], h_ref[...], NT, preferred_element_type=F32)
    cosines = cos_ref[...]
    sines = sin_ref[...]

    def rotate(base):
        first = qkv[base:base + half]
        second = qkv[base + half:base + head_dim]
        return jnp.concatenate([first * cosines - second * sines, second * cosines + first * sines], axis=0)

    scale = head_dim ** -0.5
    for head in range(heads):
        base = head * head_dim
        q_sc[head] = (rotate(base).astype(BF16).astype(F32) * scale).astype(BF16)
        k_sc[tile, head] = rotate(width + base).T.astype(BF16)
    v_sc[tile] = qkv[2 * width:3 * width].astype(BF16)
    m_sc[...] = jnp.full(m_sc.shape, NEG, F32)
    l_sc[...] = jnp.zeros(l_sc.shape, F32)
    acc_sc[...] = jnp.zeros(acc_sc.shape, F32)

    def block(key_tile, masked):
        if masked:
            key_index = key_tile * rows + lax.broadcasted_iota(jnp.int32, (rows, rows), 0)
            query_index = tile * rows + lax.broadcasted_iota(jnp.int32, (1, rows), 1)
            allowed = (key_index >= start_ref[...]) & (key_index <= query_index)
        for head in range(heads):
            scores = jnp.dot(k_sc[key_tile, head], q_sc[head], preferred_element_type=F32)
            if masked:
                scores = jnp.where(allowed, scores, NEG)
            old_max = m_sc[head]
            new_max = jnp.maximum(old_max, jnp.max(scores, axis=0, keepdims=True))
            prob = jnp.exp(scores - new_max)
            fade = jnp.exp(old_max - new_max)
            m_sc[head] = new_max
            l_sc[head] = fade * l_sc[head] + jnp.sum(prob, axis=0, keepdims=True)
            part = jnp.dot(v_sc[key_tile, head * head_dim:(head + 1) * head_dim], prob.astype(BF16), preferred_element_type=F32)
            acc_sc[head] = acc_sc[head] * fade + part

    def masked_step(key_tile, carry):
        block(key_tile, True)
        return carry

    def open_step(key_tile, carry):
        block(key_tile, False)
        return carry

    first_tile = bounds_ref[0, tile]
    open_tile = bounds_ref[1, tile]
    lax.fori_loop(first_tile, open_tile, masked_step, 0)
    lax.fori_loop(open_tile, tile, open_step, 0)
    block(tile, True)
    for head in range(heads):
        out_ref[0, head * head_dim:(head + 1) * head_dim] = (acc_sc[head] / l_sc[head]).astype(BF16)


def attention(normed, w_all, layer, cosines, sines, starts, parts, heads, head_dim, rows):
    seq_len, hidden = normed.shape
    tiles = seq_len // rows
    width = heads * head_dim
    per_part = tiles // parts
    shards, _, depth, _ = w_all.shape
    first_start = starts[::rows]
    last_start = starts[rows - 1::rows]
    tile_index = jnp.arange(tiles, dtype=jnp.int32)
    bounds = jnp.stack([first_start // rows, jnp.minimum((last_start + rows - 1) // rows, tile_index)])
    grid_spec = pltpu.PrefetchScalarGridSpec(
        num_scalar_prefetch=1,
        grid=(tiles,),
        in_specs=[
            pl.BlockSpec((rows, hidden), lambda i, b: (i, 0)),
            pl.BlockSpec((shards, 1, depth, 3 * width), lambda i, b: (0, layer, 0, 0)),
            pl.BlockSpec((head_dim // 2, rows), lambda i, b: (0, i)),
            pl.BlockSpec((head_dim // 2, rows), lambda i, b: (0, i)),
            pl.BlockSpec((1, rows), lambda i, b: (0, i)),
        ],
        out_specs=pl.BlockSpec((1, width, rows), lambda i, b: (i // per_part, 0, i % per_part)),
        scratch_shapes=[
            pltpu.VMEM((3 * width, hidden), BF16),
            pltpu.VMEM((heads, head_dim, rows), BF16),
            pltpu.VMEM((tiles, heads, rows, head_dim), BF16),
            pltpu.VMEM((tiles, width, rows), BF16),
            pltpu.VMEM((heads, 1, rows), F32),
            pltpu.VMEM((heads, 1, rows), F32),
            pltpu.VMEM((heads, head_dim, rows), F32),
        ],
    )
    flops = 2 * seq_len * hidden * 3 * width + 2 * seq_len * seq_len * width
    return pl.pallas_call(
        functools.partial(attention_kernel, heads, head_dim),
        grid_spec=grid_spec,
        out_shape=jax.ShapeDtypeStruct((parts, width, seq_len // parts), BF16),
        compiler_params=pltpu.CompilerParams(dimension_semantics=('arbitrary',), vmem_limit_bytes=VMEM_LIMIT),
        cost_estimate=pl.CostEstimate(flops=flops, bytes_accessed=4 * seq_len * hidden, transcendentals=seq_len * seq_len * heads // 2),
        name='attention',
    )(bounds, normed, w_all, cosines, sines, starts[None, :])


LAYER_COPIES = 24
SLOTS = 3


def layer_kernel(layer, parts, has_next, o_hbm, wo_hbm, r_ref, gain_mlp, gain_next, ints_ref, gates_ref, gate_hbm, up_hbm, down_hbm, *rest):
    if has_next:
        res_ref, rows_all, hbuf, own_o, wo_ref, obuf, relay, wbuf, acc, inbox, route, own, send_sem, recv_sem, w_sem, local_sem = rest
    else:
        res_ref, hbuf, own_o, wo_ref, obuf, relay, wbuf, acc, inbox, route, send_sem, recv_sem, w_sem, local_sem = rest
    me, left, right, far = ring('mp', parts)
    to_left, to_right = {'mp': left}, {'mp': right}
    wire = Wire(send_sem, recv_sem)
    _, num_experts, _, ffn = gate_hbm.shape
    width = o_hbm.shape[1]
    tokens, hidden = res_ref.shape
    half = tokens // 2
    low, high = pl.ds(0, half), pl.ds(half, half)
    o_low, o_high = pl.ds(0, width // 2), pl.ds(width // 2, width // 2)

    def weight_copies(step):
        expert = lax.rem(step, num_experts)
        slot = lax.rem(step, SLOTS)
        return [pltpu.make_async_copy(hbm.at[:, expert], wbuf.at[slot, index], w_sem.at[slot, index]) for index, hbm in enumerate((gate_hbm, up_hbm, down_hbm))]

    for step in range(SLOTS - 1):
        for copy in weight_copies(step):
            copy.start()
    own_copy = pltpu.make_async_copy(o_hbm.at[me], own_o, local_sem.at[0])
    own_copy.start()
    wo_copy = pltpu.make_async_copy(wo_hbm.at[:, :, layer], wo_ref, local_sem.at[1])
    wo_copy.start()
    meet([to_left, to_right])

    exchange = [
        wire.copy(0, o_hbm.at[far, o_low], relay.at[0], to_right),
        wire.copy(1, o_hbm.at[far, o_high], relay.at[1], to_left),
        wire.copy(2, o_hbm.at[right], obuf.at[0], to_right),
        wire.copy(3, o_hbm.at[left], obuf.at[1], to_left),
        wire.copy(4, relay.at[0], obuf.at[2, o_low], to_right),
        wire.copy(5, relay.at[1], obuf.at[2, o_high], to_left),
    ]
    for copy in exchange[:4]:
        copy.start()

    expert_row = lax.broadcasted_iota(jnp.int32, (num_experts, 1), 0)
    for part in range(parts):
        share = jnp.zeros((num_experts, tokens), F32)
        for choice in range(2):
            share = share + jnp.where(ints_ref[part, 1 + choice:2 + choice] == expert_row, gates_ref[part, choice:choice + 1], 0.0)
        route[part] = share.T

    exchange[0].wait_recv()
    exchange[4].start()
    exchange[1].wait_recv()
    exchange[5].start()
    own_copy.wait()
    wo_copy.wait()
    for copy in exchange[2:]:
        copy.wait_recv()

    chunk = min(256, tokens)

    def project(index, carry):
        span = pl.ds(pl.multiple_of(index * chunk, chunk), chunk)
        total = None
        for source, piece in ((me, own_o), (left, obuf.at[0]), (right, obuf.at[1]), (far, obuf.at[2])):
            weight = wo_ref[:, source].reshape(hidden, width)
            term = jnp.dot(weight, piece[:, span], preferred_element_type=F32)
            total = term if total is None else total + term
        residual = r_ref[span].astype(F32) + total.T
        res_ref[span] = residual
        hbuf[me, span] = rms_norm(residual, gain_mlp[...])
        return carry

    lax.fori_loop(0, tokens // chunk, project, 0)

    rows = row_gather(wire, 6, hbuf.at[me], hbuf, left, right, me)
    for name in FIRST:
        rows[name].start()

    sends = {
        1: wire.copy(12, acc.at[1], inbox.at[0], to_left),
        2: wire.copy(13, acc.at[2], inbox.at[1], to_right),
        3: wire.copy(14, acc.at[3], inbox.at[2], to_right),
        4: wire.copy(15, acc.at[4], inbox.at[3], to_left),
        5: wire.copy(16, acc.at[5], inbox.at[4], to_right),
        6: wire.copy(17, acc.at[6], inbox.at[5], to_left),
    }
    tile_rows = min(256, half)
    tiles = half // tile_rows
    lane = lax.broadcasted_iota(jnp.int32, (tile_rows, num_experts), 1)
    steps = 8 * num_experts

    def expert_step(step, carry):
        phase = step // num_experts
        expert = lax.rem(step, num_experts)
        slot = lax.rem(step, SLOTS)
        late = phase // 4
        near = phase + late * (7 - 2 * phase)
        is_zero = ((3 - near) * (2 - near) * (1 - near)) // 6
        is_one = (near * (3 - near) * (2 - near)) // 2
        is_two = (near * (3 - near) * (near - 1)) // 2
        shift = near - 1 + is_zero + 3 * is_one
        source = lax.rem(me + shift, parts)
        top = is_two + late * (1 - 2 * is_two)
        start = pl.multiple_of(top * half, half)

        @pl.when(step + SLOTS - 1 < steps)
        def _():
            for copy in weight_copies(step + SLOTS - 1):
                copy.start()

        @pl.when(expert == 0)
        def _():
            acc[phase] = jnp.zeros((half, hidden), F32)

            @pl.when(phase == 1)
            def _():
                rows['right_low'].wait_recv()
                rows['on_right'].start()

            @pl.when(phase == 2)
            def _():
                sends[1].start()
                rows['left_high'].wait_recv()
                rows['on_left'].start()

            @pl.when(phase == 3)
            def _():
                sends[2].start()
                rows['on_right'].wait_recv()

            @pl.when(phase == 4)
            def _():
                sends[3].start()
                rows['on_left'].wait_recv()

            @pl.when(phase == 5)
            def _():
                sends[4].start()
                rows['left_low'].wait_recv()

            @pl.when(phase == 6)
            def _():
                rows['right_high'].wait_recv()

            @pl.when(phase == 7)
            def _():
                sends[3].wait_recv()
                acc[5] += inbox[2]
                sends[5].start()
                sends[4].wait_recv()
                acc[6] += inbox[3]
                sends[6].start()

        for copy in weight_copies(step):
            copy.wait()

        def activate(tile):
            gate_w = wbuf[slot, 0].reshape(hidden, ffn)
            up_w = wbuf[slot, 1].reshape(hidden, ffn)
            x = hbuf[source, pl.ds(start + tile * tile_rows, tile_rows)]
            gate_pre = jnp.dot(x, gate_w, preferred_element_type=F32)
            up_pre = jnp.dot(x, up_w, preferred_element_type=F32)
            return (gate_pre * (1.0 / (1.0 + jnp.exp(-gate_pre))) * up_pre).astype(BF16)

        def contract(tile, act):
            down_w = wbuf[slot, 2].reshape(hidden, ffn)
            part_share = route[source, pl.ds(start + tile * tile_rows, tile_rows)]
            share = jnp.sum(jnp.where(lane == expert, part_share, 0.0), axis=1, keepdims=True)
            mixed = lax.dot_general(act, down_w, NT, preferred_element_type=F32)
            acc[phase, tile * tile_rows:(tile + 1) * tile_rows] += share * mixed

        act = activate(0)
        for tile in range(tiles):
            following = activate(tile + 1) if tile + 1 < tiles else None
            contract(tile, act)
            act = following
        return carry

    lax.fori_loop(0, steps, expert_step, 0)

    sends[1].wait_recv()
    res_ref[low] += acc[0] + inbox[0]
    sends[2].wait_recv()
    res_ref[high] += acc[7] + inbox[1]
    sends[5].wait_recv()
    res_ref[low] += inbox[4]
    if has_next:
        own[low] = rms_norm(res_ref[low], gain_next[...])
    sends[6].wait_recv()
    res_ref[high] += inbox[5]
    for copy in exchange + list(rows.values()) + list(sends.values()):
        copy.wait_send()
    if has_next:
        own[high] = rms_norm(res_ref[high], gain_next[...])
        rows_next = row_gather(wire, 18, own, rows_all, left, right, me)
        for name in FIRST:
            rows_next[name].start()
        rows_local = pltpu.make_async_copy(own, rows_all.at[me], local_sem.at[2])
        rows_local.start()
        rows_next['right_low'].wait_recv()
        rows_next['on_right'].start()
        rows_next['left_high'].wait_recv()
        rows_next['on_left'].start()
        for name in ('right_high', 'left_low', 'on_right', 'on_left'):
            rows_next[name].wait_recv()
        for copy in rows_next.values():
            copy.wait_send()
        rows_local.wait()


def layer_rest(layer, has_next, parts, heads_out, out_all, residual, gain_mlp, gain_next, ints_all, gates_all, gate_weight, up_weight, down_weight):
    _, width, tokens = heads_out.shape
    hidden = residual.shape[1]
    shards, num_experts, depth, ffn = gate_weight.shape
    half = tokens // 2
    anywhere = pl.BlockSpec(memory_space=pl.ANY)
    vmem = pl.BlockSpec(memory_space=pltpu.VMEM)
    out_shape = [jax.ShapeDtypeStruct((tokens, hidden), F32)]
    out_specs = [vmem]
    scratch = [
        pltpu.VMEM((parts, tokens, hidden), BF16),
        pltpu.VMEM((width, tokens), BF16),
        pltpu.VMEM((shards, parts, depth, width), BF16),
        pltpu.VMEM((3, width, tokens), BF16),
        pltpu.VMEM((2, width // 2, tokens), BF16),
        pltpu.VMEM((SLOTS, 3, shards, depth, ffn), BF16),
        pltpu.VMEM((8, half, hidden), F32),
        pltpu.VMEM((6, half, hidden), F32),
        pltpu.VMEM((parts, tokens, num_experts), F32),
    ]
    if has_next:
        out_shape.append(jax.ShapeDtypeStruct((parts, tokens, hidden), BF16))
        out_specs.append(anywhere)
        scratch.append(pltpu.VMEM((tokens, hidden), BF16))
    scratch += [
        pltpu.SemaphoreType.DMA((LAYER_COPIES,)),
        pltpu.SemaphoreType.DMA((LAYER_COPIES,)),
        pltpu.SemaphoreType.DMA((SLOTS, 3)),
        pltpu.SemaphoreType.DMA((3,)),
    ]
    return pl.pallas_call(
        functools.partial(layer_kernel, layer, parts, has_next),
        in_specs=[
            anywhere, anywhere,
            vmem, vmem, vmem, vmem, vmem,
            anywhere, anywhere, anywhere,
        ],
        out_specs=out_specs,
        out_shape=out_shape,
        scratch_shapes=scratch,
        compiler_params=pltpu.CompilerParams(collective_id=1 + layer, has_side_effects=True, vmem_limit_bytes=VMEM_LIMIT),
        cost_estimate=pl.CostEstimate(
            flops=6 * parts * tokens * hidden * ffn * num_experts,
            bytes_accessed=8 * 6 * num_experts * hidden * ffn,
            transcendentals=parts * tokens * ffn * num_experts,
        ),
        name='layer_rest',
    )(heads_out, out_all, residual, gain_mlp, gain_next, ints_all, gates_all, gate_weight, up_weight, down_weight)


def solution(mesh):
    token_spec = P(('rep', 'tok', 'mp'))
    row_spec = P(('rep', 'tok', 'mp'), None)
    head_weight = P(None, 'tok', 'mp', None)
    in_specs = (row_spec, token_spec, row_spec, row_spec, head_weight, head_weight, head_weight, P(None, 'mp', None, 'tok'), P(None, None, 'tok', 'mp'), P(None, None, 'tok', 'mp'), P(None, None, 'mp', 'tok'), P(None, None), P(None, None))
    parts = mesh.shape['mp']
    shards = mesh.shape['tok']

    def device_step(hidden_in, seg_ids, expert_ids, expert_gates, w_query, w_key, w_value, w_out, w_gate, w_up, w_down, gain_attn, gain_mlp):
        num_layers, depth, heads, head_dim = w_query.shape
        tokens, hidden = hidden_in.shape
        seq_len = tokens * parts
        width = heads * head_dim

        weights = []
        for layer in range(num_layers):
            gate_weight = lax.all_gather(w_gate[layer], 'tok', axis=0)
            up_weight = lax.all_gather(w_up[layer], 'tok', axis=0)
            down_weight = lax.all_gather(jnp.swapaxes(w_down[layer], 1, 2), 'tok', axis=0)
            weights.append((gate_weight, up_weight, down_weight))

        qkv_local = jnp.concatenate([w.reshape(num_layers, depth, width) for w in (w_query, w_key, w_value)], axis=2)
        out_local = jnp.swapaxes(w_out.reshape(num_layers, width, depth), 1, 2)
        ints = jnp.concatenate([seg_ids[None, :], expert_ids.T, jnp.zeros((5, tokens), jnp.int32)], axis=0)
        gates = jnp.concatenate([expert_gates.T, jnp.zeros((6, tokens), F32)], axis=0)
        rows_all, ints_all, gates_all, qkv_all, out_all = gather_start(hidden_in, gain_attn[:1], ints, gates, qkv_local, out_local, parts, shards)

        starts = request_starts(ints_all[:, 0].reshape(seq_len))
        positions = (jnp.arange(seq_len, dtype=jnp.int32) - starts).astype(F32)
        inv_freq = jnp.power(ROPE_BASE, -jnp.arange(head_dim // 2, dtype=F32) * 2.0 / head_dim)
        angles = inv_freq[:, None] * positions[None, :]
        cosines = jnp.cos(angles)
        sines = jnp.sin(angles)

        residual = hidden_in
        for layer in range(num_layers):
            has_next = layer + 1 < num_layers
            heads_out = attention(rows_all.reshape(seq_len, hidden), qkv_all, layer, cosines, sines, starts, parts, heads, head_dim, min(512, tokens))
            following = gain_attn[layer + 1:layer + 2] if has_next else gain_attn[layer:layer + 1]
            outs = layer_rest(layer, has_next, parts, heads_out, out_all, residual, gain_mlp[layer:layer + 1], following, ints_all, gates_all, *weights[layer])
            residual = outs[0]
            rows_all = outs[1] if has_next else None
        return residual

    return jax.shard_map(device_step, mesh=mesh, in_specs=in_specs, out_specs=row_spec, check_vma=False)
```

time: 1100 us -> 706 us (0.64)
  the two profiles are of different devices: /device:TPU:97 before, /device:TPU:110 now
where the time goes in v2:
time: 706 us
  Pallas kernels  639 us (91%)
  waiting for transfers between devices  30.8 us (4%)
  local copies, waits for them, and re-layouts  16.3 us (2%)
  between operations  13.7 us (2%)
    pallas_call x2, Pallas kernels, layer_rest(): pl.pallas_call(functools.partial(layer_kernel, layer, parts, has_next), i...  456 us
    pallas_call x2, Pallas kernels, attention(): pl.pallas_call(functools.partial(attention_kernel, heads, head_dim), grid...  97.1 us
    pallas_call x1, Pallas kernels, gather_start(): pl.pallas_call(functools.partial(gather_kernel, parts, shards), in_specs=...  86.6 us
    all_gather x2, waiting for transfers between devices, device_step(): lax.all_gather(jnp.swapaxes(w_down[layer], 1, 2), 'tok', axis=0)  29 us
  transfers between devices with their start and end apart: 6, of which 1 were waited for; matrix products, arithmetic and copies ran while one was open for 2% of the time, Pallas kernels for 61%

profile of v2, /device:TPU:110, one launch (start us, length us, event | category | flops | bytes accessed | tf_op | source)
XLA Modules:
  0.0 706.0 jit_solution(15505632396552061863)
XLA Ops:
  6.6 3.4 fusion.1
  10.1 1.6 fusion.2
  11.8 3.2 slice_bitcast_fusion
  15.2 0.5 all-gather.13.cloned.1.call-update
  15.9 0.6 all-gather.15.cloned.1.call-update
  16.5 0.6 all-gather.19.cloned.1.call-update
  17.1 0.6 fusion.4
  18.1 0.7 copy.25
  18.9 0.6 concatenate.15.gates_ref
  19.5 0.8 pad_maximum_fusion.qkv_ref
  20.3 0.7 add_add_fusion.ints_ref
  21.0 86.6 %gather_start.1 = (bf16[4,1024,768]{2,1,0:T(8,128)(2,1)}, s32[4,8,1024]{2,1,0:T(8,128)}, f32[4,8,1024]{2,1,0:T(8,128)}, bf16[8,2,96,576]{3,2,1,0:T(8,128)(2,1)}, bf16[8,4,2,96,192]{4,3,2,1,0:T(8,128)(2,1)}) custom-call(bf16[1024,768]{1,0:T(8,128)(2,1)} %r_ref.1, bf16[1,768]{1,0:T(2,128)(2,1)} %get-tuple-element.32.gain_ref, s32[8,1024]{1,0:T(8,128)} %add_add_fusion.ints_ref, ...), custom_call_target="tpu_custom_call" | custom-call | flops 20000000000 | bytes 6291456 | tf_op jit(solution)/shard_map/gather_start/pallas_call | solution.py:161
  107.7 0.9 slice.56
  108.7 0.3 reduce-window.9
  109.2 0.1 slice_reduce_fusion
  109.6 0.5 pad_add_fusion.bounds_ref
  110.1 0.6 fusion.3
  110.7 2.8 multiply_sine_fusion
  113.5 48.5 %attention.2.o_hbm = bf16[4,192,1024]{2,1,0:T(8,128)(2,1)} custom-call(s32[2,8]{1,0:T(2,128)} %pad_add_fusion.bounds_ref, bf16[4096,768]{1,0:T(8,128)(2,1)} %bitcast.47, bf16[8,2,96,576]{3,2,1,0:T(8,128)(2,1)} %get-tuple-element.14.w_ref, f32[32,4096]{1,0:T(8,128)} %get-tuple-element.28.cos_ref, f32[32,4096]{1,0:T(8,128)} %get-tuple-element.27.sin_ref, ...), custom_call_target="tpu_custom_call" | custom-call | flops 10066329600 | bytes 12582912 | tf_op jit(solution)/shard_map/attention/pallas_call | solution.py:280
  162.1 29.0 %all-gather.17.cloned.1.call-done = bf16[64,96,768]{2,1,0:T(8,128)(2,1)} async-done(((bf16[8,96,768]{2,1,0:T(8,128)(2,1)}), bf16[64,96,768]{2,1,0:T(8,128)(2,1)}) %all-gather.17.cloned.1.call-update) | async-done | bytes 9437200 | tf_op jit(solution)/shard_map/all_gather | solution.py:570
  191.0 249.8 %layer_rest.2 = (f32[1024,768]{1,0:T(8,128)}, bf16[4,1024,768]{2,1,0:T(8,128)(2,1)}) custom-call(bf16[4,192,1024]{2,1,0:T(8,128)(2,1)} %attention.2.o_hbm, bf16[8,4,2,96,192]{4,3,2,1,0:T(8,128)(2,1)} %get-tuple-element.15.wo_hbm, bf16[1024,768]{1,0:T(8,128)(2,1)} %r_ref.1, bf16[1,768]{1,0:T(2,128)(2,1)} %get-tuple-element.30.gain_mlp, ...), custom_call_target="tpu_custom_call" | custom-call | flops 115964116992 | bytes 226492416 | tf_op jit(solution)/shard_map/layer_rest/pallas_call | solution.py:532
  440.8 48.6 %attention.3.o_hbm = bf16[4,192,1024]{2,1,0:T(8,128)(2,1)} custom-call(s32[2,8]{1,0:T(2,128)} %pad_add_fusion.bounds_ref, bf16[4096,768]{1,0:T(8,128)(2,1)} %bitcast.48, bf16[8,2,96,576]{3,2,1,0:T(8,128)(2,1)} %get-tuple-element.14.w_ref, f32[32,4096]{1,0:T(8,128)} %get-tuple-element.28.cos_ref, f32[32,4096]{1,0:T(8,128)} %get-tuple-element.27.sin_ref, ...), custom_call_target="tpu_custom_call" | custom-call | flops 10066329600 | bytes 12582912 | tf_op jit(solution)/shard_map/attention/pallas_call | solution.py:280
  489.4 205.9 %layer_rest.3 = f32[1024,768]{1,0:T(8,128)} custom-call(bf16[4,192,1024]{2,1,0:T(8,128)(2,1)} %attention.3.o_hbm, bf16[8,4,2,96,192]{4,3,2,1,0:T(8,128)(2,1)} %get-tuple-element.15.wo_hbm, f32[1024,768]{1,0:T(8,128)} %get-tuple-element.18.r_ref, bf16[1,768]{1,0:T(2,128)(2,1)} %get-tuple-element.29.gain_mlp, bf16[1,768]{1,0:T(2,128)(2,1)} %get-tuple-element.31.gain_next, ...), custom_call_target="tpu_custom_call" | custom-call | flops 115964116992 | bytes 226492416 | tf_op jit(solution)/shard_map/layer_rest/pallas_call | solution.py:532
  695.3 3.8 copy.27
  (50 shorter events, 1.5 us)
Async XLA Ops:
  6.5 3.5 copy-start
  6.5 155.5 %all-gather.11.cloned.1.call-start = ((), (), s32[]{:S(2)}) async-start(), calls=%async_computation.1 | async-start | bytes 10616832 | tf_op jit(solution)/shard_map/all_gather | solution.py:569
  10.0 152.1 %all-gather.9.cloned.1.call-start = ((), (), s32[]{:S(2)}) async-start(), calls=%async_computation | async-start | bytes 10616832 | tf_op jit(solution)/shard_map/all_gather | solution.py:568
  11.8 179.3 %all-gather.17.cloned.1.call-start = ((), (), s32[]{:S(2)}) async-start(), calls=%async_computation.4 | async-start | bytes 10616832 | tf_op jit(solution)/shard_map/all_gather | solution.py:570
  15.1 2.0 copy-start.6
  15.1 2.6 copy-start.1
  15.1 2.7 copy-start.2
  15.1 2.9 copy-start.3
  15.1 2.9 copy-start.4
  15.1 3.7 copy-start.8
  15.2 474.2 %all-gather.13.cloned.1.call-start = ((), (), s32[]{:S(2)}) async-start(), calls=%async_computation.2 | async-start | bytes 10616832 | tf_op jit(solution)/shard_map/all_gather | solution.py:568
  15.2 5.1 copy-start.9
  15.2 5.1 copy-start.10
  15.8 473.6 %all-gather.15.cloned.1.call-start = ((), (), s32[]{:S(2)}) async-start(), calls=%async_computation.3 | async-start | bytes 10616832 | tf_op jit(solution)/shard_map/all_gather | solution.py:569
  16.4 473.0 %all-gather.19.cloned.1.call-start = ((), (), s32[]{:S(2)}) async-start(), calls=%async_computation.5 | async-start | bytes 10616832 | tf_op jit(solution)/shard_map/all_gather | solution.py:570
  21.0 89.1 %copy-start.7 = (bf16[2,768]{1,0:T(2,128)(2,1)S(1)}, bf16[2,768]{1,0:T(2,128)(2,1)}, u32[]{:S(2)}) copy-start(bf16[2,768]{1,0:T(2,128)(2,1)} %param.25) | copy-start | bytes 9220
  109.3 4.2 copy-start.5
Sparse Core Ops, SparseCore 0:
  10.1 74.1 all-gather.10
  85.9 51.7 all-gather.8
  139.3 51.7 all-gather.16
  192.5 51.7 all-gather.12
  245.7 51.7 all-gather.14
  298.9 51.7 all-gather.18

commit v3 on v2

--- a/solution.py
+++ b/solution.py
@@ -15,6 +15,7 @@
 BF16 = jnp.bfloat16
 NT = (((1,), (1,)), ((), ()))
 MESH = pl.DeviceIdType.MESH
+AHEAD = 2
 
 
 def rms_norm(residual, gain):
@@ -49,10 +50,10 @@
     pl.semaphore_wait(barrier, len(devices))
 
 
-def row_gather(wire, base, own, rows_all, left, right, me):
+def ring_gather(wire, base, own, rows_all, axis, left, right, me):
     half = own.shape[0] // 2
     low, high = pl.ds(0, half), pl.ds(half, half)
-    to_right, to_left = {'mp': right}, {'mp': left}
+    to_right, to_left = {axis: right}, {axis: left}
     return {
         'right_low': wire.copy(base, own.at[low], rows_all.at[me, low], to_right),
         'right_high': wire.copy(base + 1, own.at[high], rows_all.at[me, high], to_right),
@@ -66,15 +67,58 @@
 FIRST = ('right_low', 'left_high', 'right_high', 'left_low')
 
 
+class ShardGather:
+    COPIES = 10
+
+    def __init__(self, wire, base, own, blocks, shards):
+        tok = lax.axis_index('tok')
+        self.left = lax.rem(tok + shards - 2, shards)
+        self.right = lax.rem(tok + 2, shards)
+        far = lax.rem(tok + shards // 2, shards)
+        partner = {'tok': tok + 1 - 2 * lax.rem(tok, 2)}
+        self.rows = ring_gather(wire, base, own, blocks, 'tok', self.left, self.right, tok)
+        self.cross = [wire.copy(base + 6, own, blocks.at[tok], partner)]
+        for index, source in enumerate((self.left, self.right, far)):
+            self.cross.append(wire.copy(base + 7 + index, blocks.at[source], blocks.at[source], partner))
+        self.devices = [partner, {'tok': self.left}, {'tok': self.right}]
+
+    def start(self):
+        for name in FIRST:
+            self.rows[name].start()
+        self.cross[0].start()
+
+    def onward(self):
+        self.rows['right_low'].wait_recv()
+        self.rows['on_right'].start()
+        self.rows['left_high'].wait_recv()
+        self.rows['on_left'].start()
+
+    def share(self):
+        self.rows['right_high'].wait_recv()
+        self.cross[1].start()
+        self.rows['left_low'].wait_recv()
+        self.cross[2].start()
+        self.rows['on_right'].wait_recv()
+        self.rows['on_left'].wait_recv()
+        self.cross[3].start()
+
+    def arrive(self):
+        for copy in self.cross:
+            copy.wait_recv()
+
+    def sent(self):
+        for copy in list(self.rows.values()) + self.cross:
+            copy.wait_send()
+
+
 def gather_kernel(parts, shards, hidden_ref, gain_ref, ints_ref, gates_ref, qkv_ref, out_ref, rows_all, ints_all, gates_all, qkv_all, out_all, own, send_sem, recv_sem, local_sem):
     me, left, right, _ = ring('mp', parts)
     tok = lax.axis_index('tok')
-    partner = tok + 1 - 2 * lax.rem(tok, 2)
-    strides = [2 * step for step in range(1, shards // 2)]
-    peers = [{'tok': lax.rem(tok + stride, shards)} for stride in strides]
-    to_left, to_right, to_partner = {'mp': left}, {'mp': right}, {'tok': partner}
-    meet([to_left, to_right, to_partner] + peers)
+    to_left, to_right = {'mp': left}, {'mp': right}
     wire = Wire(send_sem, recv_sem)
+    qkv = ShardGather(wire, 15, qkv_ref, qkv_all, shards)
+    out = ShardGather(wire, 25, out_all.at[tok], out_all, shards)
+    meet([to_left, to_right] + qkv.devices)
     small = [
         wire.copy(0, out_ref, out_all.at[tok, me], to_right),
         wire.copy(1, out_ref, out_all.at[tok, me], to_left),
@@ -83,79 +127,58 @@
         wire.copy(4, gates_ref, gates_all.at[me], to_right),
         wire.copy(5, gates_ref, gates_all.at[me], to_left),
     ]
+    onward = [
+        wire.copy(6, out_all.at[tok, left], out_all.at[tok, left], to_right),
+        wire.copy(7, ints_all.at[left], ints_all.at[left], to_right),
+        wire.copy(8, gates_all.at[right], gates_all.at[right], to_left),
+    ]
     local = [
         pltpu.make_async_copy(out_ref, out_all.at[tok, me], local_sem.at[0]),
         pltpu.make_async_copy(ints_ref, ints_all.at[me], local_sem.at[1]),
         pltpu.make_async_copy(gates_ref, gates_all.at[me], local_sem.at[2]),
         pltpu.make_async_copy(qkv_ref, qkv_all.at[tok], local_sem.at[3]),
     ]
-    slot = 6
-    qkv_out = []
-    for peer in peers:
-        qkv_out.append(wire.copy(slot, qkv_ref, qkv_all.at[tok], peer))
-        slot += 1
-    qkv_cross = [wire.copy(slot, qkv_ref, qkv_all.at[tok], to_partner)]
-    slot += 1
-    for stride in strides:
-        source = lax.rem(tok + shards - stride, shards)
-        qkv_cross.append(wire.copy(slot, qkv_all.at[source], qkv_all.at[source], to_partner))
-        slot += 1
-    for copy in small + local + qkv_out + qkv_cross[:1]:
+    for copy in small + local:
         copy.start()
+    qkv.start()
     own[...] = rms_norm(hidden_ref[...].astype(F32), gain_ref[...])
-    rows = row_gather(wire, slot, own, rows_all, left, right, me)
-    slot += 6
+    rows = ring_gather(wire, 9, own, rows_all, 'mp', left, right, me)
     rows_local = pltpu.make_async_copy(own, rows_all.at[me], local_sem.at[4])
     for name in FIRST:
         rows[name].start()
     rows_local.start()
-    onward = [
-        wire.copy(slot, out_all.at[tok, left], out_all.at[tok, left], to_right),
-        wire.copy(slot + 1, ints_all.at[left], ints_all.at[left], to_right),
-        wire.copy(slot + 2, gates_all.at[right], gates_all.at[right], to_left),
-    ]
-    slot += 3
     for copy in small:
         copy.wait_recv()
     for copy in onward:
         copy.start()
-    for copy, after in zip(qkv_cross[1:], qkv_out):
-        after.wait_recv()
-        copy.start()
     onward[0].wait_recv()
     local[0].wait()
-    out_out = []
-    for peer in peers:
-        out_out.append(wire.copy(slot, out_all.at[tok], out_all.at[tok], peer))
-        slot += 1
-    out_cross = [wire.copy(slot, out_all.at[tok], out_all.at[tok], to_partner)]
-    slot += 1
-    for stride in strides:
-        source = lax.rem(tok + shards - stride, shards)
-        out_cross.append(wire.copy(slot, out_all.at[source], out_all.at[source], to_partner))
-        slot += 1
-    for copy in out_out + out_cross[:1]:
-        copy.start()
-    for copy, after in zip(out_cross[1:], out_out):
-        after.wait_recv()
-        copy.start()
+    out.start()
+    qkv.onward()
     rows['right_low'].wait_recv()
     rows['on_right'].start()
     rows['left_high'].wait_recv()
     rows['on_left'].start()
-    for copy in onward[1:] + qkv_cross + out_cross:
-        copy.wait_recv()
+    out.onward()
+    qkv.share()
+    out.share()
     for name in ('right_high', 'left_low', 'on_right', 'on_left'):
         rows[name].wait_recv()
-    for copy in small + onward + qkv_out + qkv_cross + out_out + out_cross + list(rows.values()):
+    for copy in onward[1:]:
+        copy.wait_recv()
+    qkv.arrive()
+    out.arrive()
+    for copy in small + onward + list(rows.values()):
         copy.wait_send()
+    qkv.sent()
+    out.sent()
     for copy in local[1:] + [rows_local]:
         copy.wait()
 
 
 def gather_start(hidden_in, gain, ints, gates, qkv_local, out_local, parts, shards):
     tokens, hidden = hidden_in.shape
-    copies = 6 + 2 * (shards - 2) // 2 + 1 + 6 + 3 + 2 * (shards - 2) // 2 + 1
+    copies = 15 + 2 * ShardGather.COPIES
     anywhere = pl.BlockSpec(memory_space=pl.ANY)
     vmem = pl.BlockSpec(memory_space=pltpu.VMEM)
     return pl.pallas_call(
@@ -181,11 +204,14 @@
     )(hidden_in, gain, ints, gates, qkv_local, out_local)
 
 
-def attention_kernel(heads, head_dim, bounds_ref, h_ref, w_ref, cos_ref, sin_ref, start_ref, out_ref, w_sc, q_sc, k_sc, v_sc, m_sc, l_sc, acc_sc):
+def attention_kernel(heads, head_dim, bounds_ref, h_ref, w_ref, cos_ref, sin_ref, start_ref, out_ref, w_sc, q_sc, k_sc, v_sc, m_sc, l_sc, acc_sc, s_sc):
     tile = pl.program_id(0)
     rows = h_ref.shape[0]
+    span = q_sc.shape[-1]
+    pieces = rows // span
     width = heads * head_dim
     half = head_dim // 2
+    units = [(head, piece) for head in range(heads) for piece in range(pieces)]
 
     @pl.when(tile == 0)
     def _():
@@ -203,46 +229,71 @@
     scale = head_dim ** -0.5
     for head in range(heads):
         base = head * head_dim
-        q_sc[head] = (rotate(base).astype(BF16).astype(F32) * scale).astype(BF16)
+        query = (rotate(base).astype(BF16).astype(F32) * scale).astype(BF16)
+        for piece in range(pieces):
+            q_sc[head * pieces + piece] = query[:, piece * span:(piece + 1) * span]
         k_sc[tile, head] = rotate(width + base).T.astype(BF16)
     v_sc[tile] = qkv[2 * width:3 * width].astype(BF16)
     m_sc[...] = jnp.full(m_sc.shape, NEG, F32)
     l_sc[...] = jnp.zeros(l_sc.shape, F32)
     acc_sc[...] = jnp.zeros(acc_sc.shape, F32)
-
-    def block(key_tile, masked):
-        if masked:
-            key_index = key_tile * rows + lax.broadcasted_iota(jnp.int32, (rows, rows), 0)
-            query_index = tile * rows + lax.broadcasted_iota(jnp.int32, (1, rows), 1)
-            allowed = (key_index >= start_ref[...]) & (key_index <= query_index)
-        for head in range(heads):
-            scores = jnp.dot(k_sc[key_tile, head], q_sc[head], preferred_element_type=F32)
-            if masked:
-                scores = jnp.where(allowed, scores, NEG)
-            old_max = m_sc[head]
-            new_max = jnp.maximum(old_max, jnp.max(scores, axis=0, keepdims=True))
-            prob = jnp.exp(scores - new_max)
-            fade = jnp.exp(old_max - new_max)
-            m_sc[head] = new_max
-            l_sc[head] = fade * l_sc[head] + jnp.sum(prob, axis=0, keepdims=True)
-            part = jnp.dot(v_sc[key_tile, head * head_dim:(head + 1) * head_dim], prob.astype(BF16), preferred_element_type=F32)
-            acc_sc[head] = acc_sc[head] * fade + part
-
-    def masked_step(key_tile, carry):
-        block(key_tile, True)
-        return carry
-
-    def open_step(key_tile, carry):
-        block(key_tile, False)
-        return carry
-
     first_tile = bounds_ref[0, tile]
     open_tile = bounds_ref[1, tile]
-    lax.fori_loop(first_tile, open_tile, masked_step, 0)
+
+    def score(unit, key_tile, keys):
+        head, _ = units[unit]
+        return jnp.dot(k_sc[key_tile, head, :keys], q_sc[unit], preferred_element_type=F32)
+
+    def absorb(unit, scores, key_tile, causal, bounded):
+        head, piece = units[unit]
+        keys = scores.shape[0]
+        if causal or bounded:
+            key_row = lax.broadcasted_iota(jnp.int32, (keys, span), 0)
+            allowed = None
+            if bounded:
+                allowed = key_row >= start_ref[:, piece * span:(piece + 1) * span] - key_tile * rows
+            if causal:
+                query_row = lax.broadcasted_iota(jnp.int32, (keys, span), 1) + piece * span
+                inside = key_row <= query_row
+                allowed = inside if allowed is None else allowed & inside
+            scores = jnp.where(allowed, scores, NEG)
+        old_max = m_sc[unit]
+        new_max = jnp.maximum(old_max, jnp.max(scores, axis=0, keepdims=True))
+        prob = jnp.exp(scores - new_max)
+        fade = jnp.exp(old_max - new_max)
+        m_sc[unit] = new_max
+        l_sc[unit] = fade * l_sc[unit] + jnp.sum(prob, axis=0, keepdims=True)
+        value = v_sc[key_tile, head * head_dim:(head + 1) * head_dim, :keys]
+        return fade, jnp.dot(value, prob.astype(BF16), preferred_element_type=F32)
+
+    def block(key_tile, diagonal, bounded):
+        def keys_of(unit):
+            return (units[unit][1] + 1) * span if diagonal else rows
+
+        waiting = [s_sc[unit, :keys_of(unit)] for unit in range(AHEAD)]
+        for unit in range(len(units)):
+            if unit + AHEAD < len(units):
+                waiting.append(score(unit + AHEAD, key_tile, keys_of(unit + AHEAD)))
+            elif not diagonal:
+                s_sc[unit + AHEAD - len(units)] = score(unit + AHEAD - len(units), key_tile + 1, rows)
+            fade, part = absorb(unit, waiting.pop(0), key_tile, diagonal, bounded)
+            acc_sc[unit] = acc_sc[unit] * fade + part
+
+    def bounded_step(key_tile, carry):
+        block(key_tile, False, True)
+        return carry
+
+    def open_step(key_tile, carry):
+        block(key_tile, False, False)
+        return carry
+
+    for unit in range(AHEAD):
+        s_sc[unit] = score(unit, first_tile, rows)
+    lax.fori_loop(first_tile, open_tile, bounded_step, 0)
     lax.fori_loop(open_tile, tile, open_step, 0)
-    block(tile, True)
-    for head in range(heads):
-        out_ref[0, head * head_dim:(head + 1) * head_dim] = (acc_sc[head] / l_sc[head]).astype(BF16)
+    block(tile, True, True)
+    for unit, (head, piece) in enumerate(units):
+        out_ref[0, head * head_dim:(head + 1) * head_dim, piece * span:(piece + 1) * span] = (acc_sc[unit] / l_sc[unit]).astype(BF16)
 
 
 def attention(normed, w_all, layer, cosines, sines, starts, parts, heads, head_dim, rows):
@@ -250,6 +301,8 @@
     tiles = seq_len // rows
     width = heads * head_dim
     per_part = tiles // parts
+    span = min(256, rows)
+    units = heads * rows // span
     shards, _, depth, _ = w_all.shape
     first_start = starts[::rows]
     last_start = starts[rows - 1::rows]
@@ -268,12 +321,13 @@
         out_specs=pl.BlockSpec((1, width, rows), lambda i, b: (i // per_part, 0, i % per_part)),
         scratch_shapes=[
             pltpu.VMEM((3 * width, hidden), BF16),
-            pltpu.VMEM((heads, head_dim, rows), BF16),
+            pltpu.VMEM((units, head_dim, span), BF16),
             pltpu.VMEM((tiles, heads, rows, head_dim), BF16),
             pltpu.VMEM((tiles, width, rows), BF16),
-            pltpu.VMEM((heads, 1, rows), F32),
-            pltpu.VMEM((heads, 1, rows), F32),
-            pltpu.VMEM((heads, head_dim, rows), F32),
+            pltpu.VMEM((units, 1, span), F32),
+            pltpu.VMEM((units, 1, span), F32),
+            pltpu.VMEM((units, head_dim, span), F32),
+            pltpu.VMEM((AHEAD, rows, span), F32),
         ],
     )
     flops = 2 * seq_len * hidden * 3 * width + 2 * seq_len * seq_len * width
@@ -287,19 +341,22 @@
     )(bounds, normed, w_all, cosines, sines, starts[None, :])
 
 
-LAYER_COPIES = 24
+LAYER_COPIES = 24 + ShardGather.COPIES
 SLOTS = 3
 
 
-def layer_kernel(layer, parts, has_next, o_hbm, wo_hbm, r_ref, gain_mlp, gain_next, ints_ref, gates_ref, gate_hbm, up_hbm, down_hbm, *rest):
-    if has_next:
+def layer_kernel(layer, parts, has_next, fetch, o_hbm, wo_hbm, r_ref, gain_mlp, gain_next, ints_ref, gates_ref, gate_hbm, up_hbm, down_hbm, *rest):
+    if fetch:
+        local_down = down_hbm
+        res_ref, rows_all, down_hbm, hbuf, own_o, wo_ref, obuf, relay, wbuf, acc, inbox, route, own, send_sem, recv_sem, w_sem, local_sem = rest
+    elif has_next:
         res_ref, rows_all, hbuf, own_o, wo_ref, obuf, relay, wbuf, acc, inbox, route, own, send_sem, recv_sem, w_sem, local_sem = rest
     else:
         res_ref, hbuf, own_o, wo_ref, obuf, relay, wbuf, acc, inbox, route, send_sem, recv_sem, w_sem, local_sem = rest
     me, left, right, far = ring('mp', parts)
     to_left, to_right = {'mp': left}, {'mp': right}
     wire = Wire(send_sem, recv_sem)
-    _, num_experts, _, ffn = gate_hbm.shape
+    shards, num_experts, _, ffn = gate_hbm.shape
     width = o_hbm.shape[1]
     tokens, hidden = res_ref.shape
     half = tokens // 2
@@ -311,14 +368,23 @@
         slot = lax.rem(step, SLOTS)
         return [pltpu.make_async_copy(hbm.at[:, expert], wbuf.at[slot, index], w_sem.at[slot, index]) for index, hbm in enumerate((gate_hbm, up_hbm, down_hbm))]
 
+    ready = 2 if fetch else 3
     for step in range(SLOTS - 1):
-        for copy in weight_copies(step):
+        for copy in weight_copies(step)[:ready]:
             copy.start()
+    devices = [to_left, to_right]
+    if fetch:
+        tok = lax.axis_index('tok')
+        down_own = wbuf.at[SLOTS - 1, 0, pl.ds(0, num_experts)]
+        down_load = pltpu.make_async_copy(local_down.at[layer], down_own, local_sem.at[3])
+        down_load.start()
+        down = ShardGather(wire, 24, down_own, down_hbm, shards)
+        devices = devices + down.devices
     own_copy = pltpu.make_async_copy(o_hbm.at[me], own_o, local_sem.at[0])
     own_copy.start()
     wo_copy = pltpu.make_async_copy(wo_hbm.at[:, :, layer], wo_ref, local_sem.at[1])
     wo_copy.start()
-    meet([to_left, to_right])
+    meet(devices)
 
     exchange = [
         wire.copy(0, o_hbm.at[far, o_low], relay.at[0], to_right),
@@ -330,6 +396,11 @@
     ]
     for copy in exchange[:4]:
         copy.start()
+    if fetch:
+        down_load.wait()
+        down.start()
+        down_store = pltpu.make_async_copy(down_own, down_hbm.at[tok], local_sem.at[4])
+        down_store.start()
 
     expert_row = lax.broadcasted_iota(jnp.int32, (num_experts, 1), 0)
     for part in range(parts):
@@ -344,6 +415,8 @@
     exchange[5].start()
     own_copy.wait()
     wo_copy.wait()
+    if fetch:
+        down.onward()
     for copy in exchange[2:]:
         copy.wait_recv()
 
@@ -363,9 +436,16 @@
 
     lax.fori_loop(0, tokens // chunk, project, 0)
 
-    rows = row_gather(wire, 6, hbuf.at[me], hbuf, left, right, me)
+    rows = ring_gather(wire, 6, hbuf.at[me], hbuf, 'mp', left, right, me)
     for name in FIRST:
         rows[name].start()
+    if fetch:
+        down.share()
+        down.arrive()
+        down.sent()
+        down_store.wait()
+        for step in range(SLOTS - 1):
+            weight_copies(step)[2].start()
 
     sends = {
         1: wire.copy(12, acc.at[1], inbox.at[0], to_left),
@@ -483,7 +563,7 @@
         copy.wait_send()
     if has_next:
         own[high] = rms_norm(res_ref[high], gain_next[...])
-        rows_next = row_gather(wire, 18, own, rows_all, left, right, me)
+        rows_next = ring_gather(wire, 18, own, rows_all, 'mp', left, right, me)
         for name in FIRST:
             rows_next[name].start()
         rows_local = pltpu.make_async_copy(own, rows_all.at[me], local_sem.at[2])
@@ -499,7 +579,7 @@
         rows_local.wait()
 
 
-def layer_rest(layer, has_next, parts, heads_out, out_all, residual, gain_mlp, gain_next, ints_all, gates_all, gate_weight, up_weight, down_weight):
+def layer_rest(layer, has_next, fetch, parts, heads_out, out_all, residual, gain_mlp, gain_next, ints_all, gates_all, gate_weight, up_weight, down_weight):
     _, width, tokens = heads_out.shape
     hidden = residual.shape[1]
     shards, num_experts, depth, ffn = gate_weight.shape
@@ -523,14 +603,17 @@
         out_shape.append(jax.ShapeDtypeStruct((parts, tokens, hidden), BF16))
         out_specs.append(anywhere)
         scratch.append(pltpu.VMEM((tokens, hidden), BF16))
+    if fetch:
+        out_shape.append(jax.ShapeDtypeStruct((shards, num_experts, depth, ffn), BF16))
+        out_specs.append(anywhere)
     scratch += [
         pltpu.SemaphoreType.DMA((LAYER_COPIES,)),
         pltpu.SemaphoreType.DMA((LAYER_COPIES,)),
         pltpu.SemaphoreType.DMA((SLOTS, 3)),
-        pltpu.SemaphoreType.DMA((3,)),
+        pltpu.SemaphoreType.DMA((5,)),
     ]
     return pl.pallas_call(
-        functools.partial(layer_kernel, layer, parts, has_next),
+        functools.partial(layer_kernel, layer, parts, has_next, fetch),
         in_specs=[
             anywhere, anywhere,
             vmem, vmem, vmem, vmem, vmem,
@@ -563,18 +646,23 @@
         seq_len = tokens * parts
         width = heads * head_dim
 
-        weights = []
-        for layer in range(num_layers):
+        def fetch(layer, w_gate, w_up, w_down):
             gate_weight = lax.all_gather(w_gate[layer], 'tok', axis=0)
             up_weight = lax.all_gather(w_up[layer], 'tok', axis=0)
-            down_weight = lax.all_gather(jnp.swapaxes(w_down[layer], 1, 2), 'tok', axis=0)
-            weights.append((gate_weight, up_weight, down_weight))
+            down_weight = lax.all_gather(jnp.swapaxes(w_down[layer], 1, 2), 'tok', axis=0) if layer else jnp.swapaxes(w_down, 2, 3)
+            return gate_weight, up_weight, down_weight
+
+        weights = [fetch(0, w_gate, w_up, w_down)]
 
         qkv_local = jnp.concatenate([w.reshape(num_layers, depth, width) for w in (w_query, w_key, w_value)], axis=2)
         out_local = jnp.swapaxes(w_out.reshape(num_layers, width, depth), 1, 2)
         ints = jnp.concatenate([seg_ids[None, :], expert_ids.T, jnp.zeros((5, tokens), jnp.int32)], axis=0)
         gates = jnp.concatenate([expert_gates.T, jnp.zeros((6, tokens), F32)], axis=0)
         rows_all, ints_all, gates_all, qkv_all, out_all = gather_start(hidden_in, gain_attn[:1], ints, gates, qkv_local, out_local, parts, shards)
+
+        ints_all, *later = lax.optimization_barrier((ints_all, w_gate, w_up, w_down))
+        for layer in range(1, num_layers):
+            weights.append(fetch(layer, *later))
 
         starts = request_starts(ints_all[:, 0].reshape(seq_len))
         positions = (jnp.arange(seq_len, dtype=jnp.int32) - starts).astype(F32)
@@ -588,7 +676,7 @@
             has_next = layer + 1 < num_layers
             heads_out = attention(rows_all.reshape(seq_len, hidden), qkv_all, layer, cosines, sines, starts, parts, heads, head_dim, min(512, tokens))
             following = gain_attn[layer + 1:layer + 2] if has_next else gain_attn[layer:layer + 1]
-            outs = layer_rest(layer, has_next, parts, heads_out, out_all, residual, gain_mlp[layer:layer + 1], following, ints_all, gates_all, *weights[layer])
+            outs = layer_rest(layer, has_next, layer == 0, parts, heads_out, out_all, residual, gain_mlp[layer:layer + 1], following, ints_all, gates_all, *weights[layer])
             residual = outs[0]
             rows_all = outs[1] if has_next else None
         return residual

time: 706 us -> 695 us (0.984)
  the two profiles are of different devices: /device:TPU:110 before, /device:TPU:111 now
where the time goes in v3:
time: 695 us
  Pallas kernels  657 us (95%)
  local copies, waits for them, and re-layouts  17.7 us (3%)
  between operations  13.4 us (2%)
    pallas_call x2, Pallas kernels, layer_rest(): pl.pallas_call(functools.partial(layer_kernel, layer, parts, has_next, fe...  505 us
    pallas_call x2, Pallas kernels, attention(): pl.pallas_call(functools.partial(attention_kernel, heads, head_dim), grid...  85.3 us
    pallas_call x1, Pallas kernels, gather_start(): pl.pallas_call(functools.partial(gather_kernel, parts, shards), in_specs=...  66.9 us
  transfers between devices with their start and end apart: 5, of which 0 were waited for; matrix products, arithmetic and copies ran while one was open for 2% of the time, Pallas kernels for 66%

profile of v3, /device:TPU:111, one launch (start us, length us, event | category | flops | bytes accessed | tf_op | source)
XLA Modules:
  0.0 694.6 jit_solution(3314628609467004457)
XLA Ops:
  6.6 2.5 slice.62
  9.3 1.1 slice.63
  10.8 0.1 copy.23
  11.0 0.7 copy.25
  11.7 0.6 concatenate.15.gates_ref
  12.3 0.8 pad_maximum_fusion.qkv_ref
  13.2 0.6 fusion.2
  13.8 0.7 add_add_fusion.ints_ref
  14.4 66.9 %gather_start.1 = (bf16[4,1024,768]{2,1,0:T(8,128)(2,1)}, s32[4,8,1024]{2,1,0:T(8,128)}, f32[4,8,1024]{2,1,0:T(8,128)}, bf16[8,2,96,576]{3,2,1,0:T(8,128)(2,1)}, bf16[8,4,2,96,192]{4,3,2,1,0:T(8,128)(2,1)}) custom-call(bf16[1024,768]{1,0:T(8,128)(2,1)} %r_ref.1, bf16[1,768]{1,0:T(2,128)(2,1)} %get-tuple-element.34.gain_ref, s32[8,1024]{1,0:T(8,128)} %add_add_fusion.ints_ref, ...), custom_call_target="tpu_custom_call" | custom-call | flops 20000000000 | bytes 6291456 | tf_op jit(solution)/shard_map/gather_start/pallas_call | solution.py:184
  81.3 2.5 slice.65
  84.0 1.1 slice.66
  85.2 0.2 all-gather.15.cloned.1.call-start
  85.4 2.4 slice_bitcast_fusion
  87.9 0.9 slice.53
  89.0 0.3 reduce-window.9
  89.4 0.1 slice_reduce_fusion
  89.8 0.6 pad_add_fusion.bounds_ref
  90.4 0.6 fusion.1
  91.0 2.8 multiply_sine_fusion
  93.8 42.6 %attention.2.o_hbm = bf16[4,192,1024]{2,1,0:T(8,128)(2,1)} custom-call(s32[2,8]{1,0:T(2,128)} %pad_add_fusion.bounds_ref, bf16[4096,768]{1,0:T(8,128)(2,1)} %bitcast.43, bf16[8,2,96,576]{3,2,1,0:T(8,128)(2,1)} %get-tuple-element.19.w_ref, f32[32,4096]{1,0:T(8,128)} %get-tuple-element.30.cos_ref, f32[32,4096]{1,0:T(8,128)} %get-tuple-element.29.sin_ref, ...), custom_call_target="tpu_custom_call" | custom-call | flops 10066329600 | bytes 12582912 | tf_op jit(solution)/shard_map/attention/pallas_call | solution.py:334
  136.4 304.5 %layer_rest.2 = (f32[1024,768]{1,0:T(8,128)}, bf16[4,1024,768]{2,1,0:T(8,128)(2,1)}, bf16[8,8,96,768]{3,2,1,0:T(8,128)(2,1)}) custom-call(bf16[4,192,1024]{2,1,0:T(8,128)(2,1)} %attention.2.o_hbm, bf16[8,4,2,96,192]{4,3,2,1,0:T(8,128)(2,1)} %get-tuple-element.20.wo_hbm, bf16[1024,768]{1,0:T(8,128)(2,1)} %r_ref.1, bf16[1,768]{1,0:T(2,128)(2,1)} %get-tuple-element.32.gain_mlp, ...), custom_call_target="tpu_custom_call" | custom-call | flops 115964116992 | bytes 226492416 | tf_op jit(solution)/shard_map/layer_rest/pallas_call | solution.py:615
  440.9 42.7 %attention.3.o_hbm = bf16[4,192,1024]{2,1,0:T(8,128)(2,1)} custom-call(s32[2,8]{1,0:T(2,128)} %pad_add_fusion.bounds_ref, bf16[4096,768]{1,0:T(8,128)(2,1)} %bitcast.44, bf16[8,2,96,576]{3,2,1,0:T(8,128)(2,1)} %get-tuple-element.19.w_ref, f32[32,4096]{1,0:T(8,128)} %get-tuple-element.30.cos_ref, f32[32,4096]{1,0:T(8,128)} %get-tuple-element.29.sin_ref, ...), custom_call_target="tpu_custom_call" | custom-call | flops 10066329600 | bytes 12582912 | tf_op jit(solution)/shard_map/attention/pallas_call | solution.py:334
  483.7 200.7 %layer_rest.3 = f32[1024,768]{1,0:T(8,128)} custom-call(bf16[4,192,1024]{2,1,0:T(8,128)(2,1)} %attention.3.o_hbm, bf16[8,4,2,96,192]{4,3,2,1,0:T(8,128)(2,1)} %get-tuple-element.20.wo_hbm, f32[1024,768]{1,0:T(8,128)} %get-tuple-element.23.r_ref, bf16[1,768]{1,0:T(2,128)(2,1)} %get-tuple-element.31.gain_mlp, bf16[1,768]{1,0:T(2,128)(2,1)} %get-tuple-element.33.gain_next, ...), custom_call_target="tpu_custom_call" | custom-call | flops 115964116992 | bytes 226492416 | tf_op jit(solution)/shard_map/layer_rest/pallas_call | solution.py:615
  684.3 3.8 copy.27
  (51 shorter events, 1.4 us)
Async XLA Ops:
  6.5 2.7 copy-start
  6.5 129.8 %all-gather.7.cloned.1.call-start = ((), (), s32[]{:S(2)}) async-start(), calls=%async_computation | async-start | bytes 10616832 | tf_op jit(solution)/shard_map/all_gather | solution.py:650
  9.1 1.6 copy-start.2
  9.1 1.7 copy-start.3
  9.1 1.8 copy-start.4
  9.1 1.9 copy-start.5
  9.1 2.6 copy-start.9
  9.2 4.0 copy-start.7
  9.2 4.6 copy-start.10
  9.2 4.6 copy-start.11
  9.2 127.2 %all-gather.9.cloned.1.call-start = ((), (), s32[]{:S(2)}) async-start(), calls=%async_computation.1 | async-start | bytes 10616832 | tf_op jit(solution)/shard_map/all_gather | solution.py:651
  10.5 473.2 %all-gather.11.cloned.1.call-start = ((), (), s32[]{:S(2)}) async-start(), calls=%async_computation.2 | async-start | bytes 10616832 | tf_op jit(solution)/shard_map/all_gather | solution.py:650
  81.3 2.7 copy-start.1
  83.9 399.7 %all-gather.13.cloned.1.call-start = ((), (), s32[]{:S(2)}) async-start(), calls=%async_computation.3 | async-start | bytes 10616832 | tf_op jit(solution)/shard_map/all_gather | solution.py:651
  85.1 5.3 copy-start.8
  85.2 398.5 %all-gather.15.cloned.1.call-start = ((), (), s32[]{:S(2)}) async-start(), calls=%async_computation.4 | async-start | bytes 10616832 | tf_op jit(solution)/shard_map/all_gather | solution.py:652
  89.6 4.2 copy-start.6
Sparse Core Ops, SparseCore 0:
  9.3 57.0 all-gather.6
  68.0 52.9 all-gather.8
  122.5 81.4 all-gather.10
  205.5 53.3 all-gather.12
  260.3 51.7 all-gather.14
